TPU v7x, 128 devices: a whole 4x4x4 slice. The times are simulated.
128 devices in a mesh: row: 16 (over y, z), col: 8 (over x, core).
Axes of the slice: x: 4, y: 4, z: 4, core: 2. Of those that a mesh axis runs over, the one named last changes fastest.
Arguments:
- rhs: float32 [2, 16, 64, 512], P(None, 'row'), may hold values from -6 to 6
- inverse_t: float32 [2, 16, 512, 512], P(None, 'row', None, 'col'), may hold values from -1 to 2, as said below
- u_factors: bfloat16 [2, 16, 4, 8, 32, 512], P(None, 'row', None, 'col'), may hold values from -0.14941406 to 0.14941406
- v_factors: bfloat16 [2, 16, 4, 8, 32, 512], P(None, 'row', None, 'col'), may hold values from -0.14941406 to 0.14941406
- tile_ranks: int32 [2, 16, 4, 8], P(None, 'row', None, 'col'), may hold values from 8 to 32
Outputs:
- solved: float32 [2, 16, 64, 512], P(None, 'row')
Inputs may be any that keep to these rules, and one draw needn't show every extreme that they name: `inverse_t`: each transposed inverse is nonsingular and of order one.
All inputs are finite; a program needn't handle non-finite values.
Results may differ from a plain program's by a relative error of at most 0.004.
Values may be sent and summed in bfloat16 or wider, within the bound.
A program may use at most 64 MiB of HBM per device.

v0:
```python
import jax
import jax.numpy as jnp
from jax import lax
from jax.sharding import PartitionSpec as P


def sent_to_all(array, axis):
    count = lax.axis_size(axis)
    return lax.all_to_all(
        jnp.broadcast_to(array[None], (count, *array.shape)), axis, 0, 0, tiled=True
    )


def taken_together(array, axis):
    everything = sent_to_all(array, axis)
    return jnp.sum(everything.astype(jnp.float32), axis=0)


def picked(array, axis, root):
    return lax.dynamic_index_in_dim(lax.all_gather(array, axis), root, 0, keepdims=False)


def laid_out(parts, dim):
    dims = list(parts.shape[1:])
    dims[dim] *= parts.shape[0]
    return jnp.moveaxis(parts, 0, dim).reshape(dims)


def gather_directly(array, axis, dim):
    return laid_out(sent_to_all(array, axis), dim)


def pick(array, index, axis):
    return lax.dynamic_index_in_dim(array, index, axis, keepdims=False)


def on_device(rhs, inverse_t, u_factors, v_factors, tile_ranks):
    rhs_here = rhs[:, 0]
    slots = rhs_here.shape[0]
    rank_width = u_factors.shape[4]
    n_row = lax.axis_size("row")
    n_col = lax.axis_size("col")
    blocks = slots * n_row
    my_row = lax.axis_index("row")
    my_col = lax.axis_index("col")
    global_rows = jnp.arange(slots, dtype=jnp.int32) * n_row + my_row
    rank_cols = lax.broadcasted_iota(jnp.int32, (1, 1, rank_width), 2)
    start = jnp.zeros(rhs_here.shape, jnp.float32)

    def apply_update(totals, full, u_col, v_col, ranks, active):
        seg_b = full.astype(jnp.bfloat16)
        proj = jnp.einsum("rb,akb->ark", seg_b, v_col, preferred_element_type=jnp.float32)
        keep = (rank_cols < ranks[:, None, None]) & active[:, None, None]
        proj_b = jnp.where(keep, proj, 0.0).astype(jnp.bfloat16)
        update = jnp.einsum("ark,akb->arb", proj_b, u_col, preferred_element_type=jnp.float32)
        return totals + update

    inverse_here = inverse_t[:, 0]
    u_here = u_factors[:, 0, :, 0]
    v_here = v_factors[:, 0, :, 0]
    ranks_here = tile_ranks[:, 0, :, 0]

    def step(k, carry):
        totals, solved = carry
        k_slot = k // n_row
        k_row = k % n_row
        c_slot = k // n_col
        c_dev = k % n_col
        summed = taken_together(pick(totals, k_slot, 0).astype(jnp.bfloat16), "col").astype(
            jnp.float32
        )
        segment = pick(rhs_here, k_slot, 0) - summed
        piece = jnp.dot(
            segment,
            pick(inverse_here, k_slot, 0),
            precision=lax.Precision.HIGHEST,
            preferred_element_type=jnp.float32,
        )
        spread = picked(piece, "row", k_row)
        full = gather_directly(spread, "col", 1)
        previous = pick(solved, k_slot, 0)
        solved = lax.dynamic_update_index_in_dim(
            solved, jnp.where(my_row == k_row, full, previous), k_slot, 0
        )
        u_col = pick(u_here, c_slot, 1)
        v_col = pick(v_here, c_slot, 1)
        ranks = pick(ranks_here, c_slot, 1)
        active = (global_rows > k) & (my_col == c_dev)
        totals = apply_update(totals, full, u_col, v_col, ranks, active)
        return (totals, solved)

    totals, solved = lax.fori_loop(0, blocks, step, (start, start))
    return solved[:, None]


def solution(mesh):
    in_specs = (
        P(None, "row", None, None),
        P(None, "row", None, "col"),
        P(None, "row", None, "col", None, None),
        P(None, "row", None, "col", None, None),
        P(None, "row", None, "col"),
    )
    out_specs = P(None, "row", None, None)
    return jax.shard_map(
        on_device, mesh=mesh, in_specs=in_specs, out_specs=out_specs, check_vma=False
    )
```

profile of v0, /device:TPU:27, one launch (start us, length us, event | category | flops | bytes accessed | tf_op | source)
XLA Modules:
  0.0 1617.6 jit_solution(18132583975353733162)
XLA Ops:
  2.3 1614.5 %while.21 = (s32[]{:T(128)}, f32[2,64,512]{2,1,0:T(8,128)S(1)}, f32[2,64,512]{2,1,0:T(8,128)S(1)}, s32[2,4]{0,1:T(4,128)S(1)}, s32[]{:T(128)}, /*index=5*/bf16[2...) while((s32[]{:T(128)}, f32[2,64,512]{2,1,0:T(8,128)S(1)}, ...), condition=%wide.region_2.3_spmd.clone.clone.clone, body=%wide.region_0.2_spmd.clone.clone.clone.sunk | while | flops 34283668 | bytes 7752926 | solution.py:92
  17.0 19.8 %all-gather.5 = f32[1024,64]{1,0:T(8,128)S(1)} all-gather(f32[64,64]{1,0:T(8,128)S(1)} %fusion.39), channel_id=2, replica_groups=mesh['row'=16,'col'=8] {'row'}, dimensions={0}, use_global_device_ids=true | all-gather | bytes 278528 | tf_op jit(solution)/shard_map/while/body/eval_jaxpr/all_gather | solution.py:20
  69.9 16.5 %all-gather.5 = f32[1024,64]{1,0:T(8,128)S(1)} all-gather(f32[64,64]{1,0:T(8,128)S(1)} %fusion.39), channel_id=2, replica_groups=mesh['row'=16,'col'=8] {'row'}, dimensions={0}, use_global_device_ids=true | all-gather | bytes 278528 | tf_op jit(solution)/shard_map/while/body/eval_jaxpr/all_gather | solution.py:20
  119.5 18.1 %all-gather.5 = f32[1024,64]{1,0:T(8,128)S(1)} all-gather(f32[64,64]{1,0:T(8,128)S(1)} %fusion.39), channel_id=2, replica_groups=mesh['row'=16,'col'=8] {'row'}, dimensions={0}, use_global_device_ids=true | all-gather | bytes 278528 | tf_op jit(solution)/shard_map/while/body/eval_jaxpr/all_gather | solution.py:20
  138.4 10.7 all-to-all-start.1
  170.8 16.4 %all-gather.5 = f32[1024,64]{1,0:T(8,128)S(1)} all-gather(f32[64,64]{1,0:T(8,128)S(1)} %fusion.39), channel_id=2, replica_groups=mesh['row'=16,'col'=8] {'row'}, dimensions={0}, use_global_device_ids=true | all-gather | bytes 278528 | tf_op jit(solution)/shard_map/while/body/eval_jaxpr/all_gather | solution.py:20
  220.3 18.1 %all-gather.5 = f32[1024,64]{1,0:T(8,128)S(1)} all-gather(f32[64,64]{1,0:T(8,128)S(1)} %fusion.39), channel_id=2, replica_groups=mesh['row'=16,'col'=8] {'row'}, dimensions={0}, use_global_device_ids=true | all-gather | bytes 278528 | tf_op jit(solution)/shard_map/while/body/eval_jaxpr/all_gather | solution.py:20
  239.3 10.7 all-to-all-start.1
  271.7 16.3 %all-gather.5 = f32[1024,64]{1,0:T(8,128)S(1)} all-gather(f32[64,64]{1,0:T(8,128)S(1)} %fusion.39), channel_id=2, replica_groups=mesh['row'=16,'col'=8] {'row'}, dimensions={0}, use_global_device_ids=true | all-gather | bytes 278528 | tf_op jit(solution)/shard_map/while/body/eval_jaxpr/all_gather | solution.py:20
  321.1 18.1 %all-gather.5 = f32[1024,64]{1,0:T(8,128)S(1)} all-gather(f32[64,64]{1,0:T(8,128)S(1)} %fusion.39), channel_id=2, replica_groups=mesh['row'=16,'col'=8] {'row'}, dimensions={0}, use_global_device_ids=true | all-gather | bytes 278528 | tf_op jit(solution)/shard_map/while/body/eval_jaxpr/all_gather | solution.py:20
  340.1 10.7 all-to-all-start.1
  372.5 16.2 %all-gather.5 = f32[1024,64]{1,0:T(8,128)S(1)} all-gather(f32[64,64]{1,0:T(8,128)S(1)} %fusion.39), channel_id=2, replica_groups=mesh['row'=16,'col'=8] {'row'}, dimensions={0}, use_global_device_ids=true | all-gather | bytes 278528 | tf_op jit(solution)/shard_map/while/body/eval_jaxpr/all_gather | solution.py:20
  421.9 18.1 %all-gather.5 = f32[1024,64]{1,0:T(8,128)S(1)} all-gather(f32[64,64]{1,0:T(8,128)S(1)} %fusion.39), channel_id=2, replica_groups=mesh['row'=16,'col'=8] {'row'}, dimensions={0}, use_global_device_ids=true | all-gather | bytes 278528 | tf_op jit(solution)/shard_map/while/body/eval_jaxpr/all_gather | solution.py:20
  440.9 10.7 all-to-all-start.1
  473.3 16.2 %all-gather.5 = f32[1024,64]{1,0:T(8,128)S(1)} all-gather(f32[64,64]{1,0:T(8,128)S(1)} %fusion.39), channel_id=2, replica_groups=mesh['row'=16,'col'=8] {'row'}, dimensions={0}, use_global_device_ids=true | all-gather | bytes 278528 | tf_op jit(solution)/shard_map/while/body/eval_jaxpr/all_gather | solution.py:20
  522.7 18.1 %all-gather.5 = f32[1024,64]{1,0:T(8,128)S(1)} all-gather(f32[64,64]{1,0:T(8,128)S(1)} %fusion.39), channel_id=2, replica_groups=mesh['row'=16,'col'=8] {'row'}, dimensions={0}, use_global_device_ids=true | all-gather | bytes 278528 | tf_op jit(solution)/shard_map/while/body/eval_jaxpr/all_gather | solution.py:20
  541.7 10.7 all-to-all-start.1
  574.1 16.2 %all-gather.5 = f32[1024,64]{1,0:T(8,128)S(1)} all-gather(f32[64,64]{1,0:T(8,128)S(1)} %fusion.39), channel_id=2, replica_groups=mesh['row'=16,'col'=8] {'row'}, dimensions={0}, use_global_device_ids=true | all-gather | bytes 278528 | tf_op jit(solution)/shard_map/while/body/eval_jaxpr/all_gather | solution.py:20
  623.6 18.1 %all-gather.5 = f32[1024,64]{1,0:T(8,128)S(1)} all-gather(f32[64,64]{1,0:T(8,128)S(1)} %fusion.39), channel_id=2, replica_groups=mesh['row'=16,'col'=8] {'row'}, dimensions={0}, use_global_device_ids=true | all-gather | bytes 278528 | tf_op jit(solution)/shard_map/while/body/eval_jaxpr/all_gather | solution.py:20
  642.5 10.7 all-to-all-start.1
  675.0 16.2 %all-gather.5 = f32[1024,64]{1,0:T(8,128)S(1)} all-gather(f32[64,64]{1,0:T(8,128)S(1)} %fusion.39), channel_id=2, replica_groups=mesh['row'=16,'col'=8] {'row'}, dimensions={0}, use_global_device_ids=true | all-gather | bytes 278528 | tf_op jit(solution)/shard_map/while/body/eval_jaxpr/all_gather | solution.py:20
  724.4 18.1 %all-gather.5 = f32[1024,64]{1,0:T(8,128)S(1)} all-gather(f32[64,64]{1,0:T(8,128)S(1)} %fusion.39), channel_id=2, replica_groups=mesh['row'=16,'col'=8] {'row'}, dimensions={0}, use_global_device_ids=true | all-gather | bytes 278528 | tf_op jit(solution)/shard_map/while/body/eval_jaxpr/all_gather | solution.py:20
  743.4 10.7 all-to-all-start.1
  775.8 16.2 %all-gather.5 = f32[1024,64]{1,0:T(8,128)S(1)} all-gather(f32[64,64]{1,0:T(8,128)S(1)} %fusion.39), channel_id=2, replica_groups=mesh['row'=16,'col'=8] {'row'}, dimensions={0}, use_global_device_ids=true | all-gather | bytes 278528 | tf_op jit(solution)/shard_map/while/body/eval_jaxpr/all_gather | solution.py:20
  825.2 18.1 %all-gather.5 = f32[1024,64]{1,0:T(8,128)S(1)} all-gather(f32[64,64]{1,0:T(8,128)S(1)} %fusion.39), channel_id=2, replica_groups=mesh['row'=16,'col'=8] {'row'}, dimensions={0}, use_global_device_ids=true | all-gather | bytes 278528 | tf_op jit(solution)/shard_map/while/body/eval_jaxpr/all_gather | solution.py:20
  844.2 10.7 all-to-all-start.1
  876.6 16.2 %all-gather.5 = f32[1024,64]{1,0:T(8,128)S(1)} all-gather(f32[64,64]{1,0:T(8,128)S(1)} %fusion.39), channel_id=2, replica_groups=mesh['row'=16,'col'=8] {'row'}, dimensions={0}, use_global_device_ids=true | all-gather | bytes 278528 | tf_op jit(solution)/shard_map/while/body/eval_jaxpr/all_gather | solution.py:20
  926.0 18.1 %all-gather.5 = f32[1024,64]{1,0:T(8,128)S(1)} all-gather(f32[64,64]{1,0:T(8,128)S(1)} %fusion.39), channel_id=2, replica_groups=mesh['row'=16,'col'=8] {'row'}, dimensions={0}, use_global_device_ids=true | all-gather | bytes 278528 | tf_op jit(solution)/shard_map/while/body/eval_jaxpr/all_gather | solution.py:20
  945.0 10.7 all-to-all-start.1
  977.4 16.2 %all-gather.5 = f32[1024,64]{1,0:T(8,128)S(1)} all-gather(f32[64,64]{1,0:T(8,128)S(1)} %fusion.39), channel_id=2, replica_groups=mesh['row'=16,'col'=8] {'row'}, dimensions={0}, use_global_device_ids=true | all-gather | bytes 278528 | tf_op jit(solution)/shard_map/while/body/eval_jaxpr/all_gather | solution.py:20
  1026.9 18.1 %all-gather.5 = f32[1024,64]{1,0:T(8,128)S(1)} all-gather(f32[64,64]{1,0:T(8,128)S(1)} %fusion.39), channel_id=2, replica_groups=mesh['row'=16,'col'=8] {'row'}, dimensions={0}, use_global_device_ids=true | all-gather | bytes 278528 | tf_op jit(solution)/shard_map/while/body/eval_jaxpr/all_gather | solution.py:20
  1045.8 10.7 all-to-all-start.1
  1078.2 16.2 %all-gather.5 = f32[1024,64]{1,0:T(8,128)S(1)} all-gather(f32[64,64]{1,0:T(8,128)S(1)} %fusion.39), channel_id=2, replica_groups=mesh['row'=16,'col'=8] {'row'}, dimensions={0}, use_global_device_ids=true | all-gather | bytes 278528 | tf_op jit(solution)/shard_map/while/body/eval_jaxpr/all_gather | solution.py:20
  1127.7 18.1 %all-gather.5 = f32[1024,64]{1,0:T(8,128)S(1)} all-gather(f32[64,64]{1,0:T(8,128)S(1)} %fusion.39), channel_id=2, replica_groups=mesh['row'=16,'col'=8] {'row'}, dimensions={0}, use_global_device_ids=true | all-gather | bytes 278528 | tf_op jit(solution)/shard_map/while/body/eval_jaxpr/all_gather | solution.py:20
  1146.7 10.7 all-to-all-start.1
  1179.1 16.2 %all-gather.5 = f32[1024,64]{1,0:T(8,128)S(1)} all-gather(f32[64,64]{1,0:T(8,128)S(1)} %fusion.39), channel_id=2, replica_groups=mesh['row'=16,'col'=8] {'row'}, dimensions={0}, use_global_device_ids=true | all-gather | bytes 278528 | tf_op jit(solution)/shard_map/while/body/eval_jaxpr/all_gather | solution.py:20
  1228.5 18.1 %all-gather.5 = f32[1024,64]{1,0:T(8,128)S(1)} all-gather(f32[64,64]{1,0:T(8,128)S(1)} %fusion.39), channel_id=2, replica_groups=mesh['row'=16,'col'=8] {'row'}, dimensions={0}, use_global_device_ids=true | all-gather | bytes 278528 | tf_op jit(solution)/shard_map/while/body/eval_jaxpr/all_gather | solution.py:20
  1247.5 10.7 all-to-all-start.1
  1279.9 16.2 %all-gather.5 = f32[1024,64]{1,0:T(8,128)S(1)} all-gather(f32[64,64]{1,0:T(8,128)S(1)} %fusion.39), channel_id=2, replica_groups=mesh['row'=16,'col'=8] {'row'}, dimensions={0}, use_global_device_ids=true | all-gather | bytes 278528 | tf_op jit(solution)/shard_map/while/body/eval_jaxpr/all_gather | solution.py:20
  1329.3 18.1 %all-gather.5 = f32[1024,64]{1,0:T(8,128)S(1)} all-gather(f32[64,64]{1,0:T(8,128)S(1)} %fusion.39), channel_id=2, replica_groups=mesh['row'=16,'col'=8] {'row'}, dimensions={0}, use_global_device_ids=true | all-gather | bytes 278528 | tf_op jit(solution)/shard_map/while/body/eval_jaxpr/all_gather | solution.py:20
  1348.3 10.7 all-to-all-start.1
  1380.7 16.2 %all-gather.5 = f32[1024,64]{1,0:T(8,128)S(1)} all-gather(f32[64,64]{1,0:T(8,128)S(1)} %fusion.39), channel_id=2, replica_groups=mesh['row'=16,'col'=8] {'row'}, dimensions={0}, use_global_device_ids=true | all-gather | bytes 278528 | tf_op jit(solution)/shard_map/while/body/eval_jaxpr/all_gather | solution.py:20
  1430.1 18.1 %all-gather.5 = f32[1024,64]{1,0:T(8,128)S(1)} all-gather(f32[64,64]{1,0:T(8,128)S(1)} %fusion.39), channel_id=2, replica_groups=mesh['row'=16,'col'=8] {'row'}, dimensions={0}, use_global_device_ids=true | all-gather | bytes 278528 | tf_op jit(solution)/shard_map/while/body/eval_jaxpr/all_gather | solution.py:20
  1449.1 10.7 all-to-all-start.1
  1481.5 16.2 %all-gather.5 = f32[1024,64]{1,0:T(8,128)S(1)} all-gather(f32[64,64]{1,0:T(8,128)S(1)} %fusion.39), channel_id=2, replica_groups=mesh['row'=16,'col'=8] {'row'}, dimensions={0}, use_global_device_ids=true | all-gather | bytes 278528 | tf_op jit(solution)/shard_map/while/body/eval_jaxpr/all_gather | solution.py:20
  1531.0 18.1 %all-gather.5 = f32[1024,64]{1,0:T(8,128)S(1)} all-gather(f32[64,64]{1,0:T(8,128)S(1)} %fusion.39), channel_id=2, replica_groups=mesh['row'=16,'col'=8] {'row'}, dimensions={0}, use_global_device_ids=true | all-gather | bytes 278528 | tf_op jit(solution)/shard_map/while/body/eval_jaxpr/all_gather | solution.py:20
  1549.9 10.7 all-to-all-start.1
  1582.3 16.2 %all-gather.5 = f32[1024,64]{1,0:T(8,128)S(1)} all-gather(f32[64,64]{1,0:T(8,128)S(1)} %fusion.39), channel_id=2, replica_groups=mesh['row'=16,'col'=8] {'row'}, dimensions={0}, use_global_device_ids=true | all-gather | bytes 278528 | tf_op jit(solution)/shard_map/while/body/eval_jaxpr/all_gather | solution.py:20
  (798 shorter events, 901.7 us)
Async XLA Ops:
  37.6 14.8 all-to-all-start.1
  55.9 13.6 all-to-all-start
  87.3 14.7 all-to-all-start.1
  105.5 13.6 all-to-all-start
  138.4 14.9 all-to-all-start.1
  156.8 13.6 all-to-all-start
  188.1 14.7 all-to-all-start.1
  206.3 13.6 all-to-all-start
  239.3 14.9 all-to-all-start.1
  257.7 13.6 all-to-all-start
  288.9 14.7 all-to-all-start.1
  307.1 13.6 all-to-all-start
  340.1 14.9 all-to-all-start.1
  358.5 13.6 all-to-all-start
  389.6 14.8 all-to-all-start.1
  440.9 14.9 all-to-all-start.1
  459.3 13.6 all-to-all-start
  490.4 14.8 all-to-all-start.1
  541.7 14.9 all-to-all-start.1
  560.1 13.6 all-to-all-start
  591.2 14.8 all-to-all-start.1
  609.6 13.6 all-to-all-start
  642.5 14.9 all-to-all-start.1
  660.9 13.6 all-to-all-start
  692.0 14.8 all-to-all-start.1
  743.4 14.9 all-to-all-start.1
  792.9 14.8 all-to-all-start.1
  844.2 14.9 all-to-all-start.1
  893.7 14.8 all-to-all-start.1
  912.0 13.6 all-to-all-start
  945.0 14.9 all-to-all-start.1
  994.5 14.8 all-to-all-start.1
  1045.8 14.9 all-to-all-start.1
  1064.2 13.6 all-to-all-start
  1095.3 14.8 all-to-all-start.1
  1113.7 13.6 all-to-all-start
  1146.7 14.9 all-to-all-start.1
  1196.1 14.8 all-to-all-start.1
  1247.5 14.9 all-to-all-start.1
  1297.0 14.8 all-to-all-start.1
  1348.3 14.9 all-to-all-start.1
  1366.7 13.6 all-to-all-start
  1397.8 14.8 all-to-all-start.1
  1416.1 13.6 all-to-all-start
  1449.1 14.9 all-to-all-start.1
  1498.6 14.8 all-to-all-start.1
  1549.9 14.9 all-to-all-start.1
  1599.4 14.8 all-to-all-start.1
  (20 other events, 221.4 us)
where the time goes:
time: 1630 us; the launch traced here: 1620 us
  blocking collectives  551 us (34%)
  starting transfers between devices  511 us (31%)
  waiting for transfers between devices  397 us (24%)
  local copies, waits for them, and re-layouts  94.1 us (6%)
  other arithmetic  37.7 us (2%)
  matrix products  22.2 us (1%)
    all_gather x32, blocking collectives, picked(): lax.all_gather(array, axis)  551 us
    all_to_all x64, starting transfers between devices, sent_to_all(): lax.all_to_all(jnp.broadcast_to(array[None], (count, *array.shape)), axis...  511 us
    all_to_all x64, waiting for transfers between devices, sent_to_all(): lax.all_to_all(jnp.broadcast_to(array[None], (count, *array.shape)), axis...  397 us
  transfers between devices with their start and end apart: 64, of which 64 were waited for; matrix products, arithmetic and copies ran while one was open for 0% of the time, Pallas kernels for 0%

commit v1 on v0

v1 whole, which is shorter than its diff:
```python
import jax
import jax.numpy as jnp
from jax import lax
from jax.experimental import pallas as pl
from jax.experimental.pallas import tpu as pltpu
from jax.sharding import PartitionSpec as P

B = 512
R = 64
K = 32
BC = 4
N_ROW = 16
N_COL = 8
S = 16
W = 4 * K
CH = 4
F32 = jnp.float32
BF16 = jnp.bfloat16
MESH = pl.DeviceIdType.MESH


def nn(a, b):
    return jnp.dot(a, b, preferred_element_type=F32)


def nt(a, b):
    return lax.dot_general(a, b, (((1,), (1,)), ((), ())), preferred_element_type=F32)


def chain_place(m):
    row = ((m // 2) % 4) * 4 + 1 + m % 2
    col = (m // 8) * 2 + 1
    return row, col


def kernel(
    ranks, rhs, inv, u, v, out,
    um, invt, zp, zpb, zf,
    inv_all, u_all, v_all, z_all, w2, m2, acc, csum, p_in, p_out, c_out, c_in, pair_p,
    inv_s, u_s, v_s, zb_s, zf_s, p_s, c_s,
    inv_r, u_r, v_r, zb_r, zf_r, p_r, c_r,
):
    r = lax.axis_index("row")
    q = lax.axis_index("col")
    half = r // 2
    i2 = r % 2
    q2 = q % 2

    def is_me(row, col):
        return (row == r) & (col == q)

    def remote(src, dst, ssem, rsem, row, col):
        return pltpu.make_async_remote_copy(
            src_ref=src, dst_ref=dst, send_sem=ssem, recv_sem=rsem,
            device_id=(row, col), device_id_type=MESH,
        )

    def send(src, dst, ssem, rsem, row, col):
        me = is_me(row, col)

        @pl.when(me)
        def _():
            pltpu.make_async_copy(src, dst, rsem).start()

        @pl.when(jnp.logical_not(me))
        def _():
            remote(src, dst, ssem, rsem, row, col).start()

    def sent(src, dst, ssem, rsem, row, col):
        @pl.when(jnp.logical_not(is_me(row, col)))
        def _():
            remote(src, dst, ssem, rsem, row, col).wait_send()

    def arrived(dst, rsem):
        pltpu.make_async_copy(dst, dst, rsem).wait()

    def inv_copy(a):
        return (
            invt.at[pl.ds(a * R, R)], inv_all.at[i2, pl.ds(pl.multiple_of(q * R, R), R)],
            inv_s.at[a], inv_r.at[i2, q], *chain_place(8 * a + half),
        )

    def u_copy(a, c):
        return (
            um.at[a, c], u_all.at[4 * c + q // 2, pl.ds(pl.multiple_of((q2 * 2 + i2) * K, K), K)],
            u_s.at[a, c], u_r.at[i2, 8 * c + q], *chain_place(8 * a + half),
        )

    def v_copy(a, c):
        return (
            v.at[a, c], v_all.at[8 * a + half, pl.ds(pl.multiple_of((q2 * 2 + i2) * K, K), K)],
            v_s.at[a, c], v_r.at[q2, 16 * a + r], *chain_place(4 * c + q // 2),
        )

    def below(a, c):
        return 8 * c + q < 16 * a + r

    def zb_copy(a):
        return (zpb, z_all.at[i2, q], zb_s.at[a], zb_r.at[i2, q], *chain_place(8 * a + half))

    def zf_copy(step):
        return (zp, zf.at[q], zf_s.at[step], zf_r.at[q], r, (q + step) % N_COL)

    for c in range(BC):
        for a in range(2):
            @pl.when(below(a, c))
            def _(a=a, c=c):
                send(*v_copy(a, c))

    both = jnp.concatenate([inv[0], inv[1]], axis=1)
    invt[...] = both.T.astype(BF16)
    for a in range(2):
        send(*inv_copy(a))

    rank_rows = lax.broadcasted_iota(jnp.int32, (K, B), 0)
    for a in range(2):
        for c in range(BC):
            um[a, c] = jnp.where(rank_rows < ranks[a, c], u[a, c].astype(F32), 0.0).astype(BF16)

            @pl.when(below(a, c))
            def _(a=a, c=c):
                send(*u_copy(a, c))

    z_mine = [
        jnp.dot(rhs[a], inv[a], precision=lax.Precision.HIGHEST, preferred_element_type=F32)
        for a in range(2)
    ]
    packed = jnp.concatenate(z_mine, axis=1)
    zp[...] = packed
    zpb[...] = packed.astype(BF16)
    for a in range(2):
        send(*zb_copy(a))
    for step in range(N_COL):
        send(*zf_copy(step))

    z_level = (r % 4) - 1
    m = (q // 2) * 8 + (r // 4) * 2 + z_level
    chains = (q2 == 1) & (q < 4) & ((z_level == 0) | (z_level == 1))

    def c_copy(b2, col):
        line = (2 * m + b2) % N_ROW
        return (c_out.at[b2], c_in.at[m // 8], c_s.at[b2, col], c_r.at[m // 8], line, col)

    def p_copy(t):
        return (p_out.at[t], p_in.at[m], p_s.at[t], p_r.at[m], *chain_place(t))

    @pl.when(chains)
    def _():
        lanes = lax.broadcasted_iota(jnp.int32, (1, CH * W), 1) % W < W // 2
        rows = lax.broadcasted_iota(jnp.int32, (W, 1), 0) % (2 * K) < K
        first = (m + 1) // CH

        for b2 in range(2):
            for col in range(N_COL):
                arrived(inv_all.at[b2, pl.ds(col * R, R)], inv_r.at[b2, col])
                arrived(z_all.at[b2, col], zb_r.at[b2, col])

            @pl.loop(0, 2 * m + b2)
            def _(l, b2=b2):
                arrived(u_all.at[l // 2, pl.ds(pl.multiple_of((l % 2) * 2 * K + b2 * K, K), K)], u_r.at[b2, l])

            @pl.loop(2 * m + b2 + 1, 2 * S)
            def _(i, b2=b2):
                arrived(v_all.at[i // 2, pl.ds(pl.multiple_of(b2 * 2 * K + (i % 2) * K, K), K)], v_r.at[b2, i])

        slot = m // 8

        def slices(b2, a):
            return jnp.concatenate([z_all[b2, col][:, a * R:(a + 1) * R] for col in range(N_COL)], axis=1)

        def joined(b2):
            return jnp.where(slot == 0, slices(b2, 0).astype(F32), slices(b2, 1).astype(F32))

        v10 = v_all[m, K:2 * K]
        w10 = nn(u_all[m, K:2 * K], jnp.transpose(inv_all[1].astype(F32)).astype(BF16)).astype(BF16)
        z0 = joined(0).astype(BF16)
        inner = nn(nt(z0, v10).astype(BF16), w10)
        z1 = (joined(1) - inner).astype(BF16)
        csum[:, :B] = jnp.zeros((R, B), F32)
        csum[:, B:] = inner
        pair_p[:, :B] = z0
        pair_p[:, B:] = z1

        @pl.loop(0, m)
        def _(lb):
            ub = u_all[lb]
            wa = jnp.where(rows, nt(ub, inv_all[0]), 0.0).astype(BF16)
            mixed = nn(nt(wa, v10).astype(BF16), w10)
            wb = (jnp.where(rows, 0.0, nt(ub, inv_all[1])) - mixed).astype(BF16)
            w2[lb, :, :B] = wa
            w2[lb, :, B:] = wb

            @pl.loop(first, S // CH)
            def _(ch):
                vc = v_all[pl.ds(ch * CH, CH)].reshape(CH * W, B)
                m2[lb, ch] = jnp.where(lanes, nt(wa, vc), nt(wb, vc)).astype(BF16)

        @pl.loop(first, S // CH)
        def _(ch):
            vc = v_all[pl.ds(ch * CH, CH)].reshape(CH * W, B)
            acc[ch] = jnp.where(lanes, nt(pair_p[:, :B], vc), nt(pair_p[:, B:], vc))

        @pl.loop(0, m - 1)
        def _(lb):
            arrived(p_in.at[lb], p_r.at[lb])
            p = p_in[lb]

            @pl.loop(first, S // CH)
            def _(ch):
                acc[ch] = acc[ch] - nn(p, m2[lb, ch])

            csum[...] = csum[...] + nn(p, w2[lb])

        last = jnp.maximum(m - 1, 0)

        @pl.when(m > 0)
        def _():
            arrived(p_in.at[last], p_r.at[last])

            @pl.loop(m + 1, S)
            def _(t):
                cols = pl.ds(pl.multiple_of((t % CH) * W, W), W)
                block = acc[t // CH, :, cols] - nn(p_in[last], m2[last, t // CH, :, cols])
                p_out[t] = block.astype(BF16)
                remote(*p_copy(t)).start()

            csum[...] = csum[...] + nn(p_in[last], w2[last])

        @pl.when(m == 0)
        def _():
            @pl.loop(1, S)
            def _(t):
                cols = pl.ds(pl.multiple_of((t % CH) * W, W), W)
                p_out[t] = acc[t // CH, :, cols].astype(BF16)
                remote(*p_copy(t)).start()

        for b2 in range(2):
            c_out[b2] = csum[:, b2 * B:(b2 + 1) * B].astype(BF16)

            @pl.loop(0, N_COL)
            def _(col, b2=b2):
                send(*c_copy(b2, col))

    for col in range(N_COL):
        arrived(zf.at[col], zf_r.at[col])
    for a in range(2):
        z = jnp.concatenate([zf[col][:, a * R:(a + 1) * R] for col in range(N_COL)], axis=1)
        arrived(c_in.at[a], c_r.at[a])
        out[a] = z - c_in[a].astype(F32)

    for a in range(2):
        sent(*inv_copy(a))
        sent(*zb_copy(a))
        for c in range(BC):
            @pl.when(below(a, c))
            def _(a=a, c=c):
                sent(*u_copy(a, c))
                sent(*v_copy(a, c))
    for step in range(1, N_COL):
        sent(*zf_copy(step))

    @pl.when(chains)
    def _():
        @pl.loop(m + 1, S)
        def _(t):
            remote(*p_copy(t)).wait_send()

        for b2 in range(2):
            @pl.loop(0, N_COL)
            def _(col, b2=b2):
                sent(*c_copy(b2, col))


def on_device(rhs, inverse_t, u_factors, v_factors, tile_ranks):
    vmem = pl.BlockSpec(memory_space=pltpu.VMEM)
    dma = pltpu.SemaphoreType.DMA
    solved = pl.pallas_call(
        kernel,
        out_shape=jax.ShapeDtypeStruct((2, R, B), F32),
        in_specs=[pl.BlockSpec(memory_space=pltpu.SMEM), vmem, vmem, vmem, vmem],
        out_specs=vmem,
        scratch_shapes=[
            pltpu.VMEM((2, BC, K, B), BF16),
            pltpu.VMEM((2 * R, B), BF16),
            pltpu.VMEM((R, 2 * R), F32),
            pltpu.VMEM((R, 2 * R), BF16),
            pltpu.VMEM((N_COL, R, 2 * R), F32),
            pltpu.VMEM((2, B, B), BF16),
            pltpu.VMEM((S, W, B), BF16),
            pltpu.VMEM((S, W, B), BF16),
            pltpu.VMEM((2, N_COL, R, 2 * R), BF16),
            pltpu.VMEM((S, W, 2 * B), BF16),
            pltpu.VMEM((S, S // CH, W, CH * W), BF16),
            pltpu.VMEM((S // CH, R, CH * W), F32),
            pltpu.VMEM((R, 2 * B), F32),
            pltpu.VMEM((S, R, W), BF16),
            pltpu.VMEM((S, R, W), BF16),
            pltpu.VMEM((2, R, B), BF16),
            pltpu.VMEM((2, R, B), BF16),
            pltpu.VMEM((R, 2 * B), BF16),
            dma((2,)), dma((2, BC)), dma((2, BC)), dma((2,)), dma((N_COL,)), dma((S,)), dma((2, N_COL)),
            dma((2, N_COL)), dma((2, 2 * S)), dma((2, 2 * S)), dma((2, N_COL)), dma((N_COL,)), dma((S,)), dma((2,)),
        ],
        compiler_params=pltpu.CompilerParams(has_side_effects=True),
    )(
        tile_ranks[:, 0, :, 0], rhs[:, 0], inverse_t[:, 0], u_factors[:, 0, :, 0], v_factors[:, 0, :, 0]
    )
    return solved[:, None]


def solution(mesh):
    in_specs = (
        P(None, "row", None, None),
        P(None, "row", None, "col"),
        P(None, "row", None, "col", None, None),
        P(None, "row", None, "col", None, None),
        P(None, "row", None, "col"),
    )
    out_specs = P(None, "row", None, None)
    return jax.shard_map(
        on_device, mesh=mesh, in_specs=in_specs, out_specs=out_specs, check_vma=False
    )
```

time: 1630 us -> 84.6 us (0.05)
  the two profiles are of different devices: /device:TPU:27 before, /device:TPU:127 now
where the time goes in v1:
time: 84.6 us; the launch traced here: 84.5 us
  Pallas kernels  80.8 us (96%)
  local copies, waits for them, and re-layouts  3.61 us (4%)
    pallas_call x1, Pallas kernels, on_device(): pl.pallas_call(kernel, out_shape=jax.ShapeDtypeStruct((2, R, B), F32), in...  80.8 us
    unnamed x2, local copies, waits for them, and re-layouts  3.61 us

profile of v1, /device:TPU:127, one launch (start us, length us, event | category | flops | bytes accessed | tf_op | source)
XLA Modules:
  0.0 84.5 jit_solution(12383165721704948247)
XLA Ops:
  0.0 1.9 %copy.6 = f32[2,1,512,64]{3,2,0,1:T(8,128)} copy(f32[2,1,512,64]{2,3,1,0:T(8,128)} %param.6) | data formatting | bytes 524288 | tf_op args[1]
  1.9 80.8 %shard_map.55 = f32[2,64,512]{2,1,0:T(8,128)} custom-call(s32[2,4]{1,0:T(2,128)} %bitcast.13, f32[2,64,512]{2,1,0:T(8,128)} %bitcast.10, f32[2,512,64]{2,1,0:T(8,128)} %bitcast.8, bf16[2,4,32,512]{3,2,1,0:T(8,128)(2,1)} %bitcast.11, bf16[2,4,32,512]{3,2,1,0:T(8,128)(2,1)} %bitcast.12), custom_call_target="tpu_custom_call" | custom-call | tf_op jit(solution)/shard_map/pallas_call | solution.py:277
  82.8 1.7 %copy.9 = f32[2,1,64,512]{3,2,1,0:T(8,128)} copy(f32[2,1,64,512]{3,2,1,0:T(8,128)} %bitcast.9) | data formatting | bytes 524288

commit v2 on v1

v2 whole, which is shorter than its diff:
```python
import jax
import jax.numpy as jnp
from jax import lax
from jax.experimental import pallas as pl
from jax.experimental.pallas import tpu as pltpu
from jax.sharding import PartitionSpec as P

B = 512
R = 64
K = 32
BC = 4
N_ROW = 16
N_COL = 8
NB = 32
T = 4
NG = NB // T
L = T * K
WIDE = L * (NG + 1)
F32 = jnp.float32
BF16 = jnp.bfloat16
MESH = pl.DeviceIdType.MESH


def nn(a, b):
    return jnp.dot(a, b, preferred_element_type=F32)


def nt(a, b, precision=None):
    return lax.dot_general(a, b, (((1,), (1,)), ((), ())), precision=precision, preferred_element_type=F32)


def row_place(j):
    x = ((j % 8) // 2 + 2 * (j // N_ROW)) % 4
    return j % N_ROW, 2 * x + 1


def chain_place(g):
    late = g // 4
    return (g % 4) * 4 + 1 + late, 2 * (1 + late) + 1


def lane_slice(g, count=1):
    return pl.ds(pl.multiple_of(g * L, L), count * L)


def kernel(
    ranks, rhs, inv, u, v, out,
    um, invt, zp, zpb, zf,
    inv_all, u_all, v_all, z_all, w, m_out, g_out, p_row, c_out, c_in,
    m_in, m_own, acc, p_in, p_out, slab,
    inv_s, u_s, v_s, zb_s, zf_s, m_s, own_s, g_s, pc_s, pr_s, c_s,
    inv_r, u_r, v_r, zb_r, zf_r, m_r, own_r, g_r, pc_r, pr_r, c_r,
):
    r = lax.axis_index("row")
    q = lax.axis_index("col")

    q_odd = q % 2 == 1
    x_here = q // 2
    late_row = jnp.where((x_here - (r % 8) // 2) % 4 == 2, 1, 0)
    j_here = r + N_ROW * late_row
    is_row = q_odd & ((x_here - (r % 8) // 2) % 2 == 0)
    g_row = j_here // T
    t_row = j_here % T
    late_chain = jnp.where(r % 4 == 2, 1, 0)
    g_here = r // 4 + 4 * late_chain
    is_chain = q_odd & (x_here == 1 + late_chain) & (r % 4 == 1 + late_chain)

    def is_me(row, col):
        return (row == r) & (col == q)

    def remote(src, dst, ssem, rsem, row, col):
        return pltpu.make_async_remote_copy(
            src_ref=src, dst_ref=dst, send_sem=ssem, recv_sem=rsem,
            device_id=(row, col), device_id_type=MESH,
        )

    def send(src, dst, ssem, rsem, row, col):
        me = is_me(row, col)

        @pl.when(me)
        def _():
            pltpu.make_async_copy(src, dst, rsem).start()

        @pl.when(jnp.logical_not(me))
        def _():
            remote(src, dst, ssem, rsem, row, col).start()

    def sent(src, dst, ssem, rsem, row, col):
        @pl.when(jnp.logical_not(is_me(row, col)))
        def _():
            remote(src, dst, ssem, rsem, row, col).wait_send()

    def arrived(dst, rsem):
        pltpu.make_async_copy(dst, dst, rsem).wait()

    barrier = pltpu.get_barrier_semaphore()

    def greet(row, col):
        @pl.when(jnp.logical_not(is_me(row, col)))
        def _():
            pl.semaphore_signal(barrier, inc=1, device_id=(row, col), device_id_type=MESH)

    for step in range(1, N_COL):
        greet(r, (q + step) % N_COL)

    @pl.when(is_row)
    def _():
        @pl.loop(0, N_ROW)
        def _(row):
            greet(row, j_here % N_COL)

        @pl.loop(0, g_row + 1)
        def _(g):
            greet(*chain_place(g))

    @pl.when(is_chain)
    def _():
        for t in range(T):
            greet(*row_place(g_here * T + t))

        @pl.loop(0, g_here)
        def _(g):
            greet(*chain_place(g))

    expected = N_COL - 1
    for c in range(BC):
        expected += jnp.where(is_me(*row_place(8 * c + q)), 0, 1)
    expected += jnp.where(is_row, 1, 0)
    expected += jnp.where(is_chain, (NG - 1 - g_here) + T * (NG - g_here), 0)

    def inv_copy(a):
        return (
            invt.at[a], inv_all.at[pl.ds(pl.multiple_of(q * R, R), R)],
            inv_s.at[a], inv_r.at[q], *row_place(N_ROW * a + r),
        )

    def u_copy(a, c):
        return (um.at[a, c], u_all.at[8 * c + q], u_s.at[a, c], u_r.at[8 * c + q], *row_place(N_ROW * a + r))

    def v_copy(a, c):
        return (v.at[a, c], v_all.at[N_ROW * a + r], v_s.at[a, c], v_r.at[N_ROW * a + r], *row_place(8 * c + q))

    def below(a, c):
        return 8 * c + q < N_ROW * a + r

    def zb_copy(a):
        return (zpb.at[a], z_all.at[q], zb_s.at[a], zb_r.at[q], *row_place(N_ROW * a + r))

    def zf_copy(step):
        return (zp, zf.at[q], zf_s.at[step], zf_r.at[q], r, (q + step) % N_COL)

    invt[...] = inv[...].astype(BF16)
    rank_rows = lax.broadcasted_iota(jnp.int32, (K, B), 0)
    for a in range(2):
        for c in range(BC):
            um[a, c] = jnp.where(rank_rows < ranks[a, c], u[a, c].astype(F32), 0.0).astype(BF16)

    pl.semaphore_wait(barrier, expected)

    for c in range(BC):
        for a in range(2):
            @pl.when(below(a, c))
            def _(a=a, c=c):
                send(*v_copy(a, c))
    for a in range(2):
        send(*inv_copy(a))
    for a in range(2):
        for c in range(BC):
            @pl.when(below(a, c))
            def _(a=a, c=c):
                send(*u_copy(a, c))

    z_mine = [nt(rhs[a], inv[a], lax.Precision.HIGHEST) for a in range(2)]
    packed = jnp.concatenate(z_mine, axis=1)
    zp[...] = packed
    for a in range(2):
        wide = jnp.concatenate([z_mine[a], z_mine[a]], axis=1)
        keep = lax.broadcasted_iota(jnp.int32, (R, 2 * R), 1) // R == q % 2
        zpb[a] = jnp.where(keep, wide, 0.0).astype(BF16)
        send(*zb_copy(a))
    for step in range(N_COL):
        send(*zf_copy(step))

    def half_lanes(k):
        return pl.ds(2 * L * k, WIDE - L - 2 * L * k)

    def m_copy(lb, k):
        return (
            m_out.at[lb, :, half_lanes(k)], m_in.at[t_row, lb, :, half_lanes(k)],
            m_s.at[lb], m_r.at[t_row, lb], *chain_place(g_row),
        )

    def own_copy(s, k):
        return (
            m_out.at[g_row, pl.ds(s * K, K), half_lanes(k)],
            m_own.at[s, t_row, pl.ds(pl.multiple_of(t_row * K, K), K), half_lanes(k)],
            own_s.at[s], own_r.at[s, t_row], *chain_place(g_row),
        )

    def g_copy(k):
        return (
            g_out.at[:, half_lanes(k)], acc.at[t_row, :, half_lanes(k)],
            g_s.at[0], g_r.at[t_row], *chain_place(g_row),
        )

    def by_width(group, do):
        for k in range(NG // 2):
            @pl.when(group // 2 == k)
            def _(k=k):
                do(k)

    def c_copy(col):
        return (c_out, c_in.at[j_here // N_ROW], c_s.at[col], c_r.at[j_here // N_ROW], r, col)

    @pl.when(is_row)
    def _():
        @pl.loop(g_row * T, j_here + 1)
        def _(i):
            v_all[i] = jnp.zeros((K, B), BF16)

        for col in range(N_COL):
            arrived(z_all.at[col], zb_r.at[col])

        @pl.loop(j_here + 1, NB)
        def _(i):
            arrived(v_all.at[i], v_r.at[i])

        z = jnp.concatenate([z_all[2 * h] + z_all[2 * h + 1] for h in range(N_COL // 2)], axis=1)

        @pl.loop(g_row // 2, NG // 2)
        def _(h):
            cols = pl.ds(pl.multiple_of(h * 2 * L, 2 * L), 2 * L)
            g_out[:, cols] = nt(z, v_all[pl.ds(h * 2 * T, 2 * T)].reshape(2 * L, B))

        by_width(g_row, lambda k: remote(*g_copy(k)).start())

        for col in range(N_COL):
            arrived(inv_all.at[pl.ds(col * R, R)], inv_r.at[col])

        rows = lax.broadcasted_iota(jnp.int32, (L, 1), 0) // K

        @pl.loop(0, g_row + 1)
        def _(lb):
            @pl.loop(0, jnp.minimum(T, j_here - lb * T))
            def _(l):
                arrived(u_all.at[lb * T + l], u_r.at[lb * T + l])

            wl = nt(u_all[pl.ds(lb * T, T)].reshape(L, B), inv_all[...])
            wl = jnp.where(rows + lb * T < j_here, wl, 0.0).astype(BF16)
            w[lb] = wl

            @pl.loop(g_row // 2, NG // 2)
            def _(h):
                cols = pl.ds(pl.multiple_of(h * 2 * L, 2 * L), 2 * L)
                m_out[lb, :, cols] = nt(wl, v_all[pl.ds(h * 2 * T, 2 * T)].reshape(2 * L, B)).astype(BF16)

            @pl.when(lb < g_row)
            def _():
                by_width(g_row, lambda k: remote(*m_copy(lb, k)).start())

            @pl.when(lb == g_row)
            def _():
                @pl.loop(0, t_row)
                def _(s):
                    by_width(g_row, lambda k: remote(*own_copy(s, k)).start())

    def p_chain_copy(g):
        return (p_out.at[g], p_in.at[g_here], pc_s.at[g], pc_r.at[g_here], *chain_place(g))

    def p_row_copy(g, i):
        return (p_out.at[g, i], p_row.at[g_here], pr_s.at[g, i], pr_r.at[g_here], *row_place(g * T + i))

    @pl.when(is_chain)
    def _():
        quarter = lax.broadcasted_iota(jnp.int32, (R, L), 1) // K
        last = jnp.maximum(g_here - 1, 0)

        def across(parts):
            gives = []
            for i in range(T):
                row = parts[0] if i == 0 else pltpu.roll(parts[0], (L - K * i) % L, 1)
                for t in range(1, T):
                    shift = (K * (t - i)) % L
                    row = jnp.where(quarter == t, parts[t] if shift == 0 else pltpu.roll(parts[t], shift, 1), row)
                gives.append(row)
            return gives

        for s in range(T):
            for t in range(s + 1, T):
                for i in range(T):
                    if i != t:
                        m_own[s, t, i * K:(i + 1) * K, :] = jnp.zeros((K, WIDE), BF16)

        @pl.when(g_here == 0)
        def _():
            p_in[0] = jnp.zeros((T, R, L), BF16)
            for t in range(T):
                m_in[t, 0] = jnp.zeros((L, WIDE), BF16)

        def wait_g(k):
            for t in range(T):
                arrived(acc.at[t, :, half_lanes(k)], g_r.at[t])

        def wait_own(k):
            for t in range(T):
                for s in range(t):
                    arrived(m_own.at[s, t, pl.ds(t * K, K), half_lanes(k)], own_r.at[s, t])

        def wait_m(lb):
            def of(k):
                for t in range(T):
                    arrived(m_in.at[t, lb, :, half_lanes(k)], m_r.at[t, lb])

            by_width(g_here, of)

        by_width(g_here, wait_g)

        @pl.loop(0, g_here - 1)
        def _(lb):
            wait_m(lb)
            arrived(p_in.at[lb], pc_r.at[lb])

            @pl.loop(g_here // 2, NG // 2)
            def _(h):
                cols = pl.ds(pl.multiple_of(h * 2 * L, 2 * L), 2 * L)
                for t in range(T):
                    acc[t, :, cols] = acc[t, :, cols] - nn(p_in[lb, t], m_in[t, lb, :, cols])

        @pl.when(g_here > 0)
        def _():
            wait_m(last)

        by_width(g_here, wait_own)

        @pl.when(g_here > 0)
        def _():
            arrived(p_in.at[last], pc_r.at[last])

        near = lane_slice(g_here, 2)
        found, inner = [], []
        for t in range(T):
            x = acc[t, :, near] - nn(p_in[last, t], m_in[t, last, :, near])
            for s in range(t):
                x = x - nn(inner[s], m_own[s, t, :, near])
            found.append(x)
            inner.append(x[:, :L].astype(BF16))

        @pl.when(g_here < NG - 1)
        def _():
            for i, block in enumerate(across([x[:, L:] for x in found])):
                p_out[g_here + 1, i] = block.astype(BF16)
            remote(*p_chain_copy(g_here + 1)).start()

        for i, block in enumerate(across([x[:, :L] for x in found])):
            p_out[g_here, i] = jnp.where(quarter < i, block, 0.0).astype(BF16)
            remote(*p_row_copy(g_here, i)).start()

        @pl.when(g_here < NG - 1)
        def _():
            for i in range(T):
                remote(*p_row_copy(g_here + 1, i)).start()
            for t in range(T):
                slab[t] = inner[t]

        @pl.loop(g_here + 2, NG)
        def _(g):
            cols = lane_slice(g)
            far = []
            for t in range(T):
                x = acc[t, :, cols] - nn(p_in[last, t], m_in[t, last, :, cols])
                for s in range(t):
                    x = x - nn(slab[s], m_own[s, t, :, cols])
                far.append(x)
            for i, block in enumerate(across(far)):
                p_out[g, i] = block.astype(BF16)
            remote(*p_chain_copy(g)).start()
            for i in range(T):
                remote(*p_row_copy(g, i)).start()

    @pl.when(is_row)
    def _():
        def term(g):
            arrived(p_row.at[g], pr_r.at[g])
            return nn(p_row[g], w[g])

        correction = lax.fori_loop(0, g_row + 1, lambda g, total: total + term(g), jnp.zeros((R, B), F32))
        c_out[...] = correction.astype(BF16)
        for col in range(N_COL):
            send(*c_copy(col))

    for col in range(N_COL):
        arrived(zf.at[col], zf_r.at[col])
    for a in range(2):
        z = jnp.concatenate([zf[col][:, a * R:(a + 1) * R] for col in range(N_COL)], axis=1)
        arrived(c_in.at[a], c_r.at[a])
        out[a] = z - c_in[a].astype(F32)

    for a in range(2):
        sent(*inv_copy(a))
        sent(*zb_copy(a))
        for c in range(BC):
            @pl.when(below(a, c))
            def _(a=a, c=c):
                sent(*u_copy(a, c))
                sent(*v_copy(a, c))
    for step in range(1, N_COL):
        sent(*zf_copy(step))

    @pl.when(is_row)
    def _():
        by_width(g_row, lambda k: remote(*g_copy(k)).wait_send())

        @pl.loop(0, g_row)
        def _(lb):
            by_width(g_row, lambda k: remote(*m_copy(lb, k)).wait_send())

        @pl.loop(0, t_row)
        def _(s):
            by_width(g_row, lambda k: remote(*own_copy(s, k)).wait_send())

        for col in range(N_COL):
            sent(*c_copy(col))

    @pl.when(is_chain)
    def _():
        @pl.loop(g_here, NG)
        def _(g):
            for i in range(T):
                remote(*p_row_copy(g, i)).wait_send()

        @pl.loop(g_here + 1, NG)
        def _(g):
            remote(*p_chain_copy(g)).wait_send()


def on_device(rhs, inverse_t, u_factors, v_factors, tile_ranks):
    vmem = pl.BlockSpec(memory_space=pltpu.VMEM)
    dma = pltpu.SemaphoreType.DMA
    solved = pl.pallas_call(
        kernel,
        out_shape=jax.ShapeDtypeStruct((2, R, B), F32),
        in_specs=[pl.BlockSpec(memory_space=pltpu.SMEM), vmem, vmem, vmem, vmem],
        out_specs=vmem,
        scratch_shapes=[
            pltpu.VMEM((2, BC, K, B), BF16),
            pltpu.VMEM((2, R, B), BF16),
            pltpu.VMEM((R, 2 * R), F32),
            pltpu.VMEM((2, R, 2 * R), BF16),
            pltpu.VMEM((N_COL, R, 2 * R), F32),
            pltpu.VMEM((B, B), BF16),
            pltpu.VMEM((NB, K, B), BF16),
            pltpu.VMEM((NB, K, B), BF16),
            pltpu.VMEM((N_COL, R, 2 * R), BF16),
            pltpu.VMEM((NG, L, B), BF16),
            pltpu.VMEM((NG, L, WIDE), BF16),
            pltpu.VMEM((R, WIDE), F32),
            pltpu.VMEM((NG, R, L), BF16),
            pltpu.VMEM((R, B), BF16),
            pltpu.VMEM((2, R, B), BF16),
            pltpu.VMEM((T, NG, L, WIDE), BF16),
            pltpu.VMEM((T, T, L, WIDE), BF16),
            pltpu.VMEM((T, R, WIDE), F32),
            pltpu.VMEM((NG, T, R, L), BF16),
            pltpu.VMEM((NG, T, R, L), BF16),
            pltpu.VMEM((T, R, L), BF16),
            dma((2,)), dma((2, BC)), dma((2, BC)), dma((2,)), dma((N_COL,)),
            dma((NG,)), dma((T,)), dma((1,)), dma((NG,)), dma((NG, T)), dma((N_COL,)),
            dma((N_COL,)), dma((NB,)), dma((NB,)), dma((N_COL,)), dma((N_COL,)),
            dma((T, NG)), dma((T, T)), dma((T,)), dma((NG,)), dma((NG,)), dma((2,)),
        ],
        compiler_params=pltpu.CompilerParams(has_side_effects=True, collective_id=0),
    )(
        tile_ranks[:, 0, :, 0], rhs[:, 0], jnp.swapaxes(inverse_t[:, 0], 1, 2),
        u_factors[:, 0, :, 0], v_factors[:, 0, :, 0],
    )
    return solved[:, None]


def solution(mesh):
    in_specs = (
        P(None, "row", None, None),
        P(None, "row", None, "col"),
        P(None, "row", None, "col", None, None),
        P(None, "row", None, "col", None, None),
        P(None, "row", None, "col"),
    )
    out_specs = P(None, "row", None, None)
    return jax.shard_map(
        on_device, mesh=mesh, in_specs=in_specs, out_specs=out_specs, check_vma=False
    )
```

time: 84.6 us -> 69 us (0.82)
  the two profiles are of different devices: /device:TPU:127 before, /device:TPU:29 now
where the time goes in v2:
time: 69 us; the launch traced here: 68.8 us
  Pallas kernels  67.2 us (97%)
  local copies, waits for them, and re-layouts  1.67 us (2%)
    pallas_call x1, Pallas kernels, on_device(): pl.pallas_call(kernel, out_shape=jax.ShapeDtypeStruct((2, R, B), F32), in...  67.2 us
    unnamed x1, local copies, waits for them, and re-layouts  1.67 us

profile of v2, /device:TPU:29, one launch (start us, length us, event | category | flops | bytes accessed | tf_op | source)
XLA Modules:
  0.0 68.8 jit_solution(1822197874282738170)
XLA Ops:
  0.0 67.2 %shard_map.55 = f32[2,64,512]{2,1,0:T(8,128)} custom-call(s32[2,4]{1,0:T(2,128)} %bitcast.15, f32[2,64,512]{2,1,0:T(8,128)} %bitcast.11, f32[2,64,512]{2,1,0:T(8,128)} %bitcast.12, bf16[2,4,32,512]{3,2,1,0:T(8,128)(2,1)} %bitcast.13, bf16[2,4,32,512]{3,2,1,0:T(8,128)(2,1)} %bitcast.14), custom_call_target="tpu_custom_call" | custom-call | tf_op jit(solution)/shard_map/pallas_call | solution.py:439
  67.2 1.7 %copy.8 = f32[2,1,64,512]{3,2,1,0:T(8,128)} copy(f32[2,1,64,512]{3,2,1,0:T(8,128)} %bitcast.10) | data formatting | bytes 524288

commit v3 on v2

v3 whole, which is shorter than its diff:
```python
import jax
import jax.numpy as jnp
from jax import lax
from jax.experimental import pallas as pl
from jax.experimental.pallas import tpu as pltpu
from jax.sharding import PartitionSpec as P

B = 512
R = 64
K = 32
BC = 4
N_ROW = 16
N_COL = 8
NB = 32
T = 4
NG = NB // T
L = T * K
NEAR = 3
WIDE = L * (NG + 2)
F32 = jnp.float32
BF16 = jnp.bfloat16
MESH = pl.DeviceIdType.MESH


def nn(a, b):
    return jnp.dot(a, b, preferred_element_type=F32)


def nt(a, b, precision=None):
    return lax.dot_general(a, b, (((1,), (1,)), ((), ())), precision=precision, preferred_element_type=F32)


def row_place(j):
    x = ((j % 8) // 2 + 2 * (j // N_ROW)) % 4
    return j % N_ROW, 2 * x + 1


def chain_place(g):
    late = g // 4
    return (g % 4) * 4 + 1 + late, 2 * (1 + late) + 1


def kernel(
    ranks, rhs_hbm, inv_hbm, u_hbm, v_hbm, out,
    rhs, inv, u, v, um, invt, zp, zpb, zf,
    inv_all, u_all, v_all, z_all, w, m_out, g_out, p_row, s_out, c_out, c_in,
    m_in, m_own, acc, s_in, p_in, p_out,
    in_s, inv_s, u_s, v_s, zb_s, zf_s, m_s, own_s, g_s, s_s, pc_s, pr_s, relay_s, c_s,
    inv_r, u_r, v_r, zb_r, zf_r, m_r, own_r, g_r, s_r, pc_r, pr_r, c_r,
):
    r = lax.axis_index("row")
    q = lax.axis_index("col")

    q_odd = q % 2 == 1
    x_here = q // 2
    late_row = jnp.where((x_here - (r % 8) // 2) % 4 == 2, 1, 0)
    j_here = r + N_ROW * late_row
    is_row = q_odd & ((x_here - (r % 8) // 2) % 2 == 0)
    g_row = j_here // T
    t_row = j_here % T
    late_chain = jnp.where(r % 4 == 2, 1, 0)
    g_here = r // 4 + 4 * late_chain
    is_chain = q_odd & (x_here == 1 + late_chain) & (r % 4 == 1 + late_chain)

    def is_me(row, col):
        return (row == r) & (col == q)

    def remote(src, dst, ssem, rsem, row, col):
        return pltpu.make_async_remote_copy(
            src_ref=src, dst_ref=dst, send_sem=ssem, recv_sem=rsem,
            device_id=(row, col), device_id_type=MESH,
        )

    def send(src, dst, ssem, rsem, row, col):
        me = is_me(row, col)

        @pl.when(me)
        def _():
            pltpu.make_async_copy(src, dst, rsem).start()

        @pl.when(jnp.logical_not(me))
        def _():
            remote(src, dst, ssem, rsem, row, col).start()

    def sent(src, dst, ssem, rsem, row, col):
        @pl.when(jnp.logical_not(is_me(row, col)))
        def _():
            remote(src, dst, ssem, rsem, row, col).wait_send()

    def arrived(dst, rsem):
        pltpu.make_async_copy(dst, dst, rsem).wait()

    barrier = pltpu.get_barrier_semaphore()

    def greet(row, col):
        @pl.when(jnp.logical_not(is_me(row, col)))
        def _():
            pl.semaphore_signal(barrier, inc=1, device_id=(row, col), device_id_type=MESH)

    for step in range(1, N_COL):
        greet(r, (q + step) % N_COL)

    @pl.when(is_row)
    def _():
        @pl.loop(0, N_ROW)
        def _(row):
            greet(row, j_here % N_COL)

        @pl.loop(jnp.maximum(g_row - NEAR + 1, 0), g_row + 1)
        def _(g):
            greet(*chain_place(g))

    @pl.when(is_chain)
    def _():
        for t in range(T):
            greet(*row_place(g_here * T + t))

        @pl.loop(jnp.maximum(g_here - NEAR + 1, 0), g_here)
        def _(g):
            greet(*chain_place(g))

        @pl.loop(0, T * (g_here - NEAR + 1))
        def _(j):
            greet(*row_place(j))

    expected = N_COL - 1
    for c in range(BC):
        expected += jnp.where(is_me(*row_place(8 * c + q)), 0, 1)
    expected += jnp.where(is_row, 1 + jnp.maximum(NG - NEAR - g_row, 0), 0)
    after = jnp.minimum(NEAR - 1, NG - 1 - g_here)
    expected += jnp.where(is_chain, after + T * (after + 1), 0)

    def inv_copy(a):
        return (
            invt.at[a], inv_all.at[pl.ds(pl.multiple_of(q * R, R), R)],
            inv_s.at[a], inv_r.at[q], *row_place(N_ROW * a + r),
        )

    def u_copy(a, c):
        return (um.at[a, c], u_all.at[8 * c + q], u_s.at[a, c], u_r.at[8 * c + q], *row_place(N_ROW * a + r))

    def v_copy(a, c):
        return (v.at[a, c], v_all.at[N_ROW * a + r], v_s.at[a, c], v_r.at[N_ROW * a + r], *row_place(8 * c + q))

    def below(a, c):
        return 8 * c + q < N_ROW * a + r

    def zb_copy(a):
        return (zpb.at[a], z_all.at[q], zb_s.at[a], zb_r.at[q], *row_place(N_ROW * a + r))

    def zf_copy(step):
        return (zp, zf.at[q], zf_s.at[step], zf_r.at[q], r, (q + step) % N_COL)

    loads = [
        pltpu.make_async_copy(src, dst, in_s.at[k])
        for k, (src, dst) in enumerate([(inv_hbm, inv), (rhs_hbm, rhs), (u_hbm, u), (v_hbm, v)])
    ]
    for load in loads:
        load.start()
    for load in loads:
        load.wait()
    invt[...] = inv[...].astype(BF16)
    rank_rows = lax.broadcasted_iota(jnp.int32, (K, B), 0)
    for a in range(2):
        for c in range(BC):
            um[a, c] = jnp.where(rank_rows < ranks[a, c], u[a, c].astype(F32), 0.0).astype(BF16)
    z_mine = [nt(rhs[a], inv[a], lax.Precision.HIGHEST) for a in range(2)]
    zp[...] = jnp.concatenate(z_mine, axis=1)
    for a in range(2):
        wide = jnp.concatenate([z_mine[a], z_mine[a]], axis=1)
        keep = lax.broadcasted_iota(jnp.int32, (R, 2 * R), 1) // R == q % 2
        zpb[a] = jnp.where(keep, wide, 0.0).astype(BF16)

    pl.semaphore_wait(barrier, expected)

    def near(a, c):
        return (N_ROW * a + r) // T - (8 * c + q) // T < NEAR

    def each_v(do, wanted, columns):
        for c in columns:
            for a in range(2):
                @pl.when(below(a, c) & (near(a, c) == wanted))
                def _(a=a, c=c):
                    do(*v_copy(a, c))

    def each_u(do, a):
        for c in range(BC):
            @pl.when(below(a, c))
            def _(c=c):
                do(*u_copy(a, c))

    def first_wave(do):
        do(*zb_copy(0))
        do(*zb_copy(1))
        each_v(do, True, (0, 1))
        do(*inv_copy(0))
        each_u(do, 0)

    def second_wave(do):
        each_v(do, True, (2, 3))
        do(*inv_copy(1))
        each_u(do, 1)

    first_wave(send)
    first_wave(sent)
    second_wave(send)
    each_v(send, False, range(BC))
    for step in range(N_COL):
        send(*zf_copy(step))

    def lanes_of(g, count):
        return pl.ds(pl.multiple_of(g * L, L), count * L)

    def m_copy(lb):
        lanes = lanes_of(g_row, NEAR)
        return (
            m_out.at[lb, :, lanes], m_in.at[t_row, lb, :, lanes],
            m_s.at[lb], m_r.at[t_row, lb], *chain_place(g_row),
        )

    def own_copy(s):
        lanes = lanes_of(g_row, NEAR)
        return (
            m_out.at[g_row, pl.ds(s * K, K), lanes],
            m_own.at[s, t_row, pl.ds(pl.multiple_of(t_row * K, K), K), lanes],
            own_s.at[s], own_r.at[s, t_row], *chain_place(g_row),
        )

    def g_copy():
        lanes = lanes_of(g_row, NEAR)
        return (
            g_out.at[:, lanes], acc.at[t_row, :, lanes],
            g_s.at[0], g_r.at[t_row], *chain_place(g_row),
        )

    def slab_copy(g):
        return (s_out.at[g], s_in.at[g_row, t_row], s_s.at[g], s_r.at[g_row, t_row], *chain_place(g))

    def c_copy(col):
        return (c_out, c_in.at[j_here // N_ROW], c_s.at[col], c_r.at[j_here // N_ROW], r, col)

    @pl.when(is_row)
    def _():
        here = lanes_of(g_row, NEAR)
        near_end = jnp.minimum((g_row + NEAR) * T, NB)
        rows = lax.broadcasted_iota(jnp.int32, (L, 1), 0) // K

        @pl.loop(g_row * T, j_here + 1)
        def _(i):
            v_all[i] = jnp.zeros((K, B), BF16)

        for col in range(N_COL):
            arrived(z_all.at[col], zb_r.at[col])

        @pl.loop(j_here + 1, near_end)
        def _(i):
            arrived(v_all.at[i], v_r.at[i])

        def z():
            return jnp.concatenate([z_all[2 * h] + z_all[2 * h + 1] for h in range(N_COL // 2)], axis=1)

        def v_of(g, count):
            return v_all[pl.ds(g * T, count * T)].reshape(count * L, B)

        g_out[:, here] = nt(z(), v_of(g_row, NEAR))
        remote(*g_copy()).start()

        for col in range(N_COL):
            arrived(inv_all.at[pl.ds(col * R, R)], inv_r.at[col])

        def form(lb):
            @pl.loop(0, jnp.minimum(T, j_here - lb * T))
            def _(l):
                arrived(u_all.at[lb * T + l], u_r.at[lb * T + l])

            wl = nt(u_all[pl.ds(lb * T, T)].reshape(L, B), inv_all[...])
            wl = jnp.where(rows + lb * T < j_here, wl, 0.0).astype(BF16)
            w[lb] = wl
            m_out[lb, :, here] = nt(wl, v_of(g_row, NEAR)).astype(BF16)

        form(g_row)

        @pl.loop(0, t_row)
        def _(s):
            remote(*own_copy(s)).start()

        @pl.loop(0, g_row)
        def _(lb):
            form(lb)
            remote(*m_copy(lb)).start()

        @pl.loop(near_end, NB)
        def _(i):
            arrived(v_all.at[i], v_r.at[i])

        @pl.loop(0, (NG - NEAR + 1 - g_row) // 2)
        def _(h):
            far = g_row + NEAR + 2 * h
            cols = lanes_of(far, 2)
            g_out[:, cols] = nt(z(), v_of(far, 2))

            @pl.loop(0, g_row + 1)
            def _(lb):
                m_out[lb, :, cols] = nt(w[lb], v_of(far, 2)).astype(BF16)

    def p_chain_copy(g):
        return (p_out.at[g], p_in.at[g_here], pc_s.at[g], pc_r.at[g_here], *chain_place(g))

    def p_row_copy(g, i):
        return (p_out.at[g, i], p_row.at[g_here], pr_s.at[g, i], pr_r.at[g_here], *row_place(g * T + i))

    def relay_copy(lb, i):
        return (p_in.at[lb, i], p_row.at[lb], relay_s.at[lb, i], pr_r.at[lb], *row_place(g_here * T + i))

    @pl.when(is_chain)
    def _():
        quarter = lax.broadcasted_iota(jnp.int32, (R, L), 1) // K
        last = jnp.maximum(g_here - 1, 0)

        def across(parts):
            gives = []
            for i in range(T):
                row = parts[0] if i == 0 else pltpu.roll(parts[0], (L - K * i) % L, 1)
                for t in range(1, T):
                    shift = (K * (t - i)) % L
                    row = jnp.where(quarter == t, parts[t] if shift == 0 else pltpu.roll(parts[t], shift, 1), row)
                gives.append(row)
            return gives

        for s in range(T):
            for t in range(s + 1, T):
                for i in range(T):
                    if i != t:
                        m_own[s, t, i * K:(i + 1) * K, :] = jnp.zeros((K, WIDE), BF16)

        @pl.when(g_here == 0)
        def _():
            p_in[0] = jnp.zeros((T, R, L), BF16)
            for t in range(T):
                m_in[t, 0] = jnp.zeros((L, WIDE), BF16)

        here = lanes_of(g_here, NEAR)
        now = lanes_of(g_here, 2)

        def wait_m(lb):
            for t in range(T):
                arrived(m_in.at[t, lb, :, here], m_r.at[t, lb])

        def update(lb):
            wait_m(lb)
            for t in range(T):
                acc[t, :, here] = acc[t, :, here] - nn(p_in[lb, t], m_in[t, lb, :, here])

        for t in range(T):
            arrived(acc.at[t, :, here], g_r.at[t])
            for s in range(t):
                arrived(m_own.at[s, t, pl.ds(t * K, K), here], own_r.at[s, t])

        @pl.loop(0, g_here - NEAR + 1)
        def _(lb):
            for t in range(T):
                arrived(s_in.at[lb, t], s_r.at[lb, t])
            for i, block in enumerate(across([s_in[lb, t].astype(F32) for t in range(T)])):
                p_in[lb, i] = block.astype(BF16)
            for i in range(T):
                remote(*relay_copy(lb, i)).start()
            update(lb)

        @pl.when(g_here > 1)
        def _():
            arrived(p_in.at[g_here - 2], pc_r.at[g_here - 2])
            update(g_here - 2)

        @pl.when(g_here > 0)
        def _():
            wait_m(last)
            arrived(p_in.at[last], pc_r.at[last])

        found, inner = [], []
        for t in range(T):
            x = acc[t, :, now] - nn(p_in[last, t], m_in[t, last, :, now])
            for s in range(t):
                x = x - nn(inner[s], m_own[s, t, :, now])
            found.append(x)
            inner.append(x[:, :L].astype(BF16))

        @pl.when(g_here < NG - 1)
        def _():
            for i, block in enumerate(across([x[:, L:] for x in found])):
                p_out[g_here + 1, i] = block.astype(BF16)
            remote(*p_chain_copy(g_here + 1)).start()

        for i, block in enumerate(across([x[:, :L] for x in found])):
            p_out[g_here, i] = jnp.where(quarter < i, block, 0.0).astype(BF16)
            remote(*p_row_copy(g_here, i)).start()

        @pl.when(g_here < NG - 1)
        def _():
            for i in range(T):
                remote(*p_row_copy(g_here + 1, i)).start()

        @pl.when(g_here < NG - 2)
        def _():
            cols = lanes_of(g_here + 2, 1)
            later = []
            for t in range(T):
                x = acc[t, :, cols] - nn(p_in[last, t], m_in[t, last, :, cols])
                for s in range(t):
                    x = x - nn(inner[s], m_own[s, t, :, cols])
                later.append(x)
            for i, block in enumerate(across(later)):
                p_out[g_here + 2, i] = block.astype(BF16)
            remote(*p_chain_copy(g_here + 2)).start()
            for i in range(T):
                remote(*p_row_copy(g_here + 2, i)).start()

    @pl.when(is_row)
    def _():
        def term(g):
            arrived(p_row.at[g], pr_r.at[g])
            p = p_row[g]

            @pl.loop(0, (NG - NEAR + 1 - g_row) // 2)
            def _(h):
                cols = lanes_of(g_row + NEAR + 2 * h, 2)
                g_out[:, cols] = g_out[:, cols] - nn(p, m_out[g, :, cols])

            @pl.when(g == g_row)
            def _():
                @pl.loop(g_row + NEAR, NG)
                def _(far):
                    s_out[far] = g_out[:, lanes_of(far, 1)].astype(BF16)
                    remote(*slab_copy(far)).start()

            return nn(p, w[g])

        correction = lax.fori_loop(0, g_row + 1, lambda g, total: total + term(g), jnp.zeros((R, B), F32))
        c_out[...] = correction.astype(BF16)
        for step in (3, 4, 1, 2, 5, 6, 7, 0):
            send(*c_copy((q + step) % N_COL))

    for col in range(N_COL):
        arrived(zf.at[col], zf_r.at[col])
    for a in range(2):
        z = jnp.concatenate([zf[col][:, a * R:(a + 1) * R] for col in range(N_COL)], axis=1)
        arrived(c_in.at[a], c_r.at[a])
        out[a] = z - c_in[a].astype(F32)

    second_wave(sent)
    each_v(sent, False, range(BC))
    for step in range(1, N_COL):
        sent(*zf_copy(step))

    @pl.when(is_row)
    def _():
        remote(*g_copy()).wait_send()

        @pl.loop(0, g_row)
        def _(lb):
            remote(*m_copy(lb)).wait_send()

        @pl.loop(0, t_row)
        def _(s):
            remote(*own_copy(s)).wait_send()

        @pl.loop(g_row + NEAR, NG)
        def _(far):
            remote(*slab_copy(far)).wait_send()

        for col in range(N_COL):
            sent(*c_copy(col))

    @pl.when(is_chain)
    def _():
        upto = jnp.minimum(g_here + NEAR, NG)

        @pl.loop(g_here, upto)
        def _(g):
            for i in range(T):
                remote(*p_row_copy(g, i)).wait_send()

        @pl.loop(g_here + 1, upto)
        def _(g):
            remote(*p_chain_copy(g)).wait_send()

        @pl.loop(0, g_here - NEAR + 1)
        def _(lb):
            for i in range(T):
                remote(*relay_copy(lb, i)).wait_send()


def on_device(rhs, inverse_t, u_factors, v_factors, tile_ranks):
    vmem = pl.BlockSpec(memory_space=pltpu.VMEM)
    hbm = pl.BlockSpec(memory_space=pl.ANY)
    dma = pltpu.SemaphoreType.DMA
    solved = pl.pallas_call(
        kernel,
        out_shape=jax.ShapeDtypeStruct((2, R, B), F32),
        in_specs=[pl.BlockSpec(memory_space=pltpu.SMEM), hbm, hbm, hbm, hbm],
        out_specs=vmem,
        scratch_shapes=[
            pltpu.VMEM((2, R, B), F32),
            pltpu.VMEM((2, R, B), F32),
            pltpu.VMEM((2, BC, K, B), BF16),
            pltpu.VMEM((2, BC, K, B), BF16),
            pltpu.VMEM((2, BC, K, B), BF16),
            pltpu.VMEM((2, R, B), BF16),
            pltpu.VMEM((R, 2 * R), F32),
            pltpu.VMEM((2, R, 2 * R), BF16),
            pltpu.VMEM((N_COL, R, 2 * R), F32),
            pltpu.VMEM((B, B), BF16),
            pltpu.VMEM((NB, K, B), BF16),
            pltpu.VMEM((NB + 2 * T, K, B), BF16),
            pltpu.VMEM((N_COL, R, 2 * R), BF16),
            pltpu.VMEM((NG, L, B), BF16),
            pltpu.VMEM((NG, L, WIDE), BF16),
            pltpu.VMEM((R, WIDE), F32),
            pltpu.VMEM((NG, R, L), BF16),
            pltpu.VMEM((NG, R, L), BF16),
            pltpu.VMEM((R, B), BF16),
            pltpu.VMEM((2, R, B), BF16),
            pltpu.VMEM((T, NG, L, WIDE), BF16),
            pltpu.VMEM((T, T, L, WIDE), BF16),
            pltpu.VMEM((T, R, WIDE), F32),
            pltpu.VMEM((NG, T, R, L), BF16),
            pltpu.VMEM((NG, T, R, L), BF16),
            pltpu.VMEM((NG, T, R, L), BF16),
            dma((4,)), dma((2,)), dma((2, BC)), dma((2, BC)), dma((2,)), dma((N_COL,)),
            dma((NG,)), dma((T,)), dma((1,)), dma((NG,)), dma((NG,)), dma((NG, T)), dma((NG, T)), dma((N_COL,)),
            dma((N_COL,)), dma((NB,)), dma((NB,)), dma((N_COL,)), dma((N_COL,)),
            dma((T, NG)), dma((T, T)), dma((T,)), dma((NG, T)), dma((NG,)), dma((NG,)), dma((2,)),
        ],
        compiler_params=pltpu.CompilerParams(has_side_effects=True, collective_id=0),
    )(
        tile_ranks[:, 0, :, 0], rhs[:, 0], jnp.swapaxes(inverse_t[:, 0], 1, 2),
        u_factors[:, 0, :, 0], v_factors[:, 0, :, 0],
    )
    return solved[:, None]


def solution(mesh):
    in_specs = (
        P(None, "row", None, None),
        P(None, "row", None, "col"),
        P(None, "row", None, "col", None, None),
        P(None, "row", None, "col", None, None),
        P(None, "row", None, "col"),
    )
    out_specs = P(None, "row", None, None)
    return jax.shard_map(
        on_device, mesh=mesh, in_specs=in_specs, out_specs=out_specs, check_vma=False
    )
```

time: 69 us -> 57 us (0.83)
  the two profiles are of different devices: /device:TPU:29 before, /device:TPU:27 now
where the time goes in v3:
time: 57 us; the launch traced here: 56.8 us
  Pallas kernels  55.2 us (97%)
  local copies, waits for them, and re-layouts  1.67 us (3%)
    pallas_call x1, Pallas kernels, on_device(): pl.pallas_call(kernel, out_shape=jax.ShapeDtypeStruct((2, R, B), F32), in...  55.2 us
    unnamed x1, local copies, waits for them, and re-layouts  1.67 us

profile of v3, /device:TPU:27, one launch (start us, length us, event | category | flops | bytes accessed | tf_op | source)
XLA Modules:
  0.0 56.8 jit_solution(16806053735279267792)
XLA Ops:
  0.0 55.2 %shard_map.55 = f32[2,64,512]{2,1,0:T(8,128)} custom-call(s32[2,4]{1,0:T(2,128)} %bitcast.15, f32[2,64,512]{2,1,0:T(8,128)} %bitcast.11, f32[2,64,512]{2,1,0:T(8,128)} %bitcast.12, bf16[2,4,32,512]{3,2,1,0:T(8,128)(2,1)} %bitcast.13, bf16[2,4,32,512]{3,2,1,0:T(8,128)(2,1)} %bitcast.14), custom_call_target="tpu_custom_call" | custom-call | tf_op jit(solution)/shard_map/pallas_call | solution.py:496
  55.2 1.7 %copy.8 = f32[2,1,64,512]{3,2,1,0:T(8,128)} copy(f32[2,1,64,512]{3,2,1,0:T(8,128)} %bitcast.10) | data formatting | bytes 524288

commit v4 on v3

--- a/solution.py
+++ b/solution.py
@@ -16,7 +16,7 @@
 NG = NB // T
 L = T * K
 NEAR = 3
-WIDE = L * (NG + 2)
+WIDE = L * (NG + NEAR - 1)
 F32 = jnp.float32
 BF16 = jnp.bfloat16
 MESH = pl.DeviceIdType.MESH
@@ -37,15 +37,15 @@
 
 def chain_place(g):
     late = g // 4
-    return (g % 4) * 4 + 1 + late, 2 * (1 + late) + 1
+    return ((g + 3 * late) % 4) * 4 + 1 + late, 2 * (1 + late) + 1
 
 
 def kernel(
-    ranks, rhs_hbm, inv_hbm, u_hbm, v_hbm, out,
+    ranks, rhs_hbm, inv_hbm, u_hbm, v_hbm, z_out, c_in,
     rhs, inv, u, v, um, invt, zp, zpb, zf,
-    inv_all, u_all, v_all, z_all, w, m_out, g_out, p_row, s_out, c_out, c_in,
+    inv_all, u_all, v_all, z_all, w, m_out, g_out, p_row, s_out, c_out, z_full,
     m_in, m_own, acc, s_in, p_in, p_out,
-    in_s, inv_s, u_s, v_s, zb_s, zf_s, m_s, own_s, g_s, s_s, pc_s, pr_s, relay_s, c_s,
+    in_s, out_s, inv_s, u_s, v_s, zb_s, zf_s, m_s, own_s, g_s, s_s, pc_s, pr_s, relay_s, c_s,
     inv_r, u_r, v_r, zb_r, zf_r, m_r, own_r, g_r, s_r, pc_r, pr_r, c_r,
 ):
     r = lax.axis_index("row")
@@ -59,7 +59,7 @@
     g_row = j_here // T
     t_row = j_here % T
     late_chain = jnp.where(r % 4 == 2, 1, 0)
-    g_here = r // 4 + 4 * late_chain
+    g_here = (r // 4 + late_chain) % 4 + 4 * late_chain
     is_chain = q_odd & (x_here == 1 + late_chain) & (r % 4 == 1 + late_chain)
 
     def is_me(row, col):
@@ -153,17 +153,13 @@
 
     loads = [
         pltpu.make_async_copy(src, dst, in_s.at[k])
-        for k, (src, dst) in enumerate([(inv_hbm, inv), (rhs_hbm, rhs), (u_hbm, u), (v_hbm, v)])
+        for k, (src, dst) in enumerate([(inv_hbm, inv), (rhs_hbm, rhs), (v_hbm, v), (u_hbm, u)])
     ]
     for load in loads:
         load.start()
-    for load in loads:
-        load.wait()
+    loads[0].wait()
     invt[...] = inv[...].astype(BF16)
-    rank_rows = lax.broadcasted_iota(jnp.int32, (K, B), 0)
-    for a in range(2):
-        for c in range(BC):
-            um[a, c] = jnp.where(rank_rows < ranks[a, c], u[a, c].astype(F32), 0.0).astype(BF16)
+    loads[1].wait()
     z_mine = [nt(rhs[a], inv[a], lax.Precision.HIGHEST) for a in range(2)]
     zp[...] = jnp.concatenate(z_mine, axis=1)
     for a in range(2):
@@ -192,42 +188,58 @@
     def first_wave(do):
         do(*zb_copy(0))
         do(*zb_copy(1))
+        do(*inv_copy(0))
         each_v(do, True, (0, 1))
-        do(*inv_copy(0))
-        each_u(do, 0)
 
     def second_wave(do):
         each_v(do, True, (2, 3))
         do(*inv_copy(1))
         each_u(do, 1)
 
+    def mask_u(a):
+        rank_rows = lax.broadcasted_iota(jnp.int32, (K, B), 0)
+        for c in range(BC):
+            um[a, c] = jnp.where(rank_rows < ranks[a, c], u[a, c].astype(F32), 0.0).astype(BF16)
+
+    loads[2].wait()
     first_wave(send)
+    loads[3].wait()
+    mask_u(0)
+    each_u(send, 0)
+    mask_u(1)
     first_wave(sent)
+    each_v(send, False, (0,))
     second_wave(send)
-    each_v(send, False, range(BC))
+    each_v(send, False, (1, 2, 3))
     for step in range(N_COL):
         send(*zf_copy(step))
 
     def lanes_of(g, count):
         return pl.ds(pl.multiple_of(g * L, L), count * L)
 
-    def m_copy(lb):
-        lanes = lanes_of(g_row, NEAR)
+    def by_width(g, do):
+        for count in range(1, NEAR + 1):
+            @pl.when(jnp.minimum(NEAR, NG - g) == count)
+            def _(count=count):
+                do(count)
+
+    def m_copy(lb, count):
+        lanes = lanes_of(g_row, count)
         return (
             m_out.at[lb, :, lanes], m_in.at[t_row, lb, :, lanes],
             m_s.at[lb], m_r.at[t_row, lb], *chain_place(g_row),
         )
 
-    def own_copy(s):
-        lanes = lanes_of(g_row, NEAR)
+    def own_copy(s, count):
+        lanes = lanes_of(g_row, count)
         return (
             m_out.at[g_row, pl.ds(s * K, K), lanes],
             m_own.at[s, t_row, pl.ds(pl.multiple_of(t_row * K, K), K), lanes],
             own_s.at[s], own_r.at[s, t_row], *chain_place(g_row),
         )
 
-    def g_copy():
-        lanes = lanes_of(g_row, NEAR)
+    def g_copy(count):
+        lanes = lanes_of(g_row, count)
         return (
             g_out.at[:, lanes], acc.at[t_row, :, lanes],
             g_s.at[0], g_r.at[t_row], *chain_place(g_row),
@@ -263,7 +275,7 @@
             return v_all[pl.ds(g * T, count * T)].reshape(count * L, B)
 
         g_out[:, here] = nt(z(), v_of(g_row, NEAR))
-        remote(*g_copy()).start()
+        by_width(g_row, lambda count: remote(*g_copy(count)).start())
 
         for col in range(N_COL):
             arrived(inv_all.at[pl.ds(col * R, R)], inv_r.at[col])
@@ -282,12 +294,12 @@
 
         @pl.loop(0, t_row)
         def _(s):
-            remote(*own_copy(s)).start()
+            by_width(g_row, lambda count: remote(*own_copy(s, count)).start())
 
         @pl.loop(0, g_row)
         def _(lb):
             form(lb)
-            remote(*m_copy(lb)).start()
+            by_width(g_row, lambda count: remote(*m_copy(lb, count)).start())
 
         @pl.loop(near_end, NB)
         def _(i):
@@ -302,6 +314,13 @@
             @pl.loop(0, g_row + 1)
             def _(lb):
                 m_out[lb, :, cols] = nt(w[lb], v_of(far, 2)).astype(BF16)
+
+    def join_z():
+        for col in range(N_COL):
+            arrived(zf.at[col], zf_r.at[col])
+        for a in range(2):
+            z_full[a] = jnp.concatenate([zf[col][:, a * R:(a + 1) * R] for col in range(N_COL)], axis=1)
+        pltpu.make_async_copy(z_full, z_out, out_s.at[0]).start()
 
     def p_chain_copy(g):
         return (p_out.at[g], p_in.at[g_here], pc_s.at[g], pc_r.at[g_here], *chain_place(g))
@@ -343,18 +362,25 @@
         now = lanes_of(g_here, 2)
 
         def wait_m(lb):
-            for t in range(T):
-                arrived(m_in.at[t, lb, :, here], m_r.at[t, lb])
+            def of(count):
+                for t in range(T):
+                    arrived(m_in.at[t, lb, :, lanes_of(g_here, count)], m_r.at[t, lb])
+
+            by_width(g_here, of)
 
         def update(lb):
             wait_m(lb)
             for t in range(T):
                 acc[t, :, here] = acc[t, :, here] - nn(p_in[lb, t], m_in[t, lb, :, here])
 
-        for t in range(T):
-            arrived(acc.at[t, :, here], g_r.at[t])
-            for s in range(t):
-                arrived(m_own.at[s, t, pl.ds(t * K, K), here], own_r.at[s, t])
+        def wait_start(count):
+            lanes = lanes_of(g_here, count)
+            for t in range(T):
+                arrived(acc.at[t, :, lanes], g_r.at[t])
+                for s in range(t):
+                    arrived(m_own.at[s, t, pl.ds(t * K, K), lanes], own_r.at[s, t])
+
+        by_width(g_here, wait_start)
 
         @pl.loop(0, g_here - NEAR + 1)
         def _(lb):
@@ -366,10 +392,10 @@
                 remote(*relay_copy(lb, i)).start()
             update(lb)
 
-        @pl.when(g_here > 1)
-        def _():
-            arrived(p_in.at[g_here - 2], pc_r.at[g_here - 2])
-            update(g_here - 2)
+        @pl.loop(jnp.maximum(g_here - NEAR + 1, 0), g_here - 1)
+        def _(lb):
+            arrived(p_in.at[lb], pc_r.at[lb])
+            update(lb)
 
         @pl.when(g_here > 0)
         def _():
@@ -391,31 +417,43 @@
             remote(*p_chain_copy(g_here + 1)).start()
 
         for i, block in enumerate(across([x[:, :L] for x in found])):
-            p_out[g_here, i] = jnp.where(quarter < i, block, 0.0).astype(BF16)
-            remote(*p_row_copy(g_here, i)).start()
+            if i > 0:
+                p_out[g_here, i] = jnp.where(quarter < i, block, 0.0).astype(BF16)
+                remote(*p_row_copy(g_here, i)).start()
 
         @pl.when(g_here < NG - 1)
         def _():
             for i in range(T):
                 remote(*p_row_copy(g_here + 1, i)).start()
 
-        @pl.when(g_here < NG - 2)
-        def _():
-            cols = lanes_of(g_here + 2, 1)
-            later = []
-            for t in range(T):
-                x = acc[t, :, cols] - nn(p_in[last, t], m_in[t, last, :, cols])
-                for s in range(t):
-                    x = x - nn(inner[s], m_own[s, t, :, cols])
-                later.append(x)
-            for i, block in enumerate(across(later)):
-                p_out[g_here + 2, i] = block.astype(BF16)
-            remote(*p_chain_copy(g_here + 2)).start()
-            for i in range(T):
-                remote(*p_row_copy(g_here + 2, i)).start()
+        for ahead in range(2, NEAR):
+            @pl.when(g_here < NG - ahead)
+            def _(ahead=ahead):
+                cols = lanes_of(g_here + ahead, 1)
+                later = []
+                for t in range(T):
+                    x = acc[t, :, cols] - nn(p_in[last, t], m_in[t, last, :, cols])
+                    for s in range(t):
+                        x = x - nn(inner[s], m_own[s, t, :, cols])
+                    later.append(x)
+                for i, block in enumerate(across(later)):
+                    p_out[g_here + ahead, i] = block.astype(BF16)
+                remote(*p_chain_copy(g_here + ahead)).start()
+                for i in range(T):
+                    remote(*p_row_copy(g_here + ahead, i)).start()
 
     @pl.when(is_row)
     def _():
+        join_z()
+
+        blocks = g_row + jnp.where(t_row > 0, 1, 0)
+
+        def send_slabs():
+            @pl.loop(g_row + NEAR, NG)
+            def _(far):
+                s_out[far] = g_out[:, lanes_of(far, 1)].astype(BF16)
+                remote(*slab_copy(far)).start()
+
         def term(g):
             arrived(p_row.at[g], pr_r.at[g])
             p = p_row[g]
@@ -425,27 +463,30 @@
                 cols = lanes_of(g_row + NEAR + 2 * h, 2)
                 g_out[:, cols] = g_out[:, cols] - nn(p, m_out[g, :, cols])
 
-            @pl.when(g == g_row)
+            @pl.when(g == blocks - 1)
             def _():
-                @pl.loop(g_row + NEAR, NG)
-                def _(far):
-                    s_out[far] = g_out[:, lanes_of(far, 1)].astype(BF16)
-                    remote(*slab_copy(far)).start()
+                send_slabs()
 
             return nn(p, w[g])
 
-        correction = lax.fori_loop(0, g_row + 1, lambda g, total: total + term(g), jnp.zeros((R, B), F32))
+        @pl.when(blocks == 0)
+        def _():
+            send_slabs()
+
+        correction = lax.fori_loop(0, blocks, lambda g, total: total + term(g), jnp.zeros((R, B), F32))
         c_out[...] = correction.astype(BF16)
         for step in (3, 4, 1, 2, 5, 6, 7, 0):
             send(*c_copy((q + step) % N_COL))
 
-    for col in range(N_COL):
-        arrived(zf.at[col], zf_r.at[col])
+    @pl.when(jnp.logical_not(is_row))
+    def _():
+        join_z()
+
+    pltpu.make_async_copy(z_full, z_out, out_s.at[0]).wait()
     for a in range(2):
-        z = jnp.concatenate([zf[col][:, a * R:(a + 1) * R] for col in range(N_COL)], axis=1)
         arrived(c_in.at[a], c_r.at[a])
-        out[a] = z - c_in[a].astype(F32)
-
+
+    each_u(sent, 0)
     second_wave(sent)
     each_v(sent, False, range(BC))
     for step in range(1, N_COL):
@@ -453,15 +494,15 @@
 
     @pl.when(is_row)
     def _():
-        remote(*g_copy()).wait_send()
+        by_width(g_row, lambda count: remote(*g_copy(count)).wait_send())
 
         @pl.loop(0, g_row)
         def _(lb):
-            remote(*m_copy(lb)).wait_send()
+            by_width(g_row, lambda count: remote(*m_copy(lb, count)).wait_send())
 
         @pl.loop(0, t_row)
         def _(s):
-            remote(*own_copy(s)).wait_send()
+            by_width(g_row, lambda count: remote(*own_copy(s, count)).wait_send())
 
         @pl.loop(g_row + NEAR, NG)
         def _(far):
@@ -474,7 +515,10 @@
     def _():
         upto = jnp.minimum(g_here + NEAR, NG)
 
-        @pl.loop(g_here, upto)
+        for i in range(1, T):
+            remote(*p_row_copy(g_here, i)).wait_send()
+
+        @pl.loop(g_here + 1, upto)
         def _(g):
             for i in range(T):
                 remote(*p_row_copy(g, i)).wait_send()
@@ -490,14 +534,13 @@
 
 
 def on_device(rhs, inverse_t, u_factors, v_factors, tile_ranks):
-    vmem = pl.BlockSpec(memory_space=pltpu.VMEM)
     hbm = pl.BlockSpec(memory_space=pl.ANY)
     dma = pltpu.SemaphoreType.DMA
-    solved = pl.pallas_call(
+    z, c = pl.pallas_call(
         kernel,
-        out_shape=jax.ShapeDtypeStruct((2, R, B), F32),
+        out_shape=(jax.ShapeDtypeStruct((2, R, B), F32), jax.ShapeDtypeStruct((2, R, B), BF16)),
         in_specs=[pl.BlockSpec(memory_space=pltpu.SMEM), hbm, hbm, hbm, hbm],
-        out_specs=vmem,
+        out_specs=(hbm, hbm),
         scratch_shapes=[
             pltpu.VMEM((2, R, B), F32),
             pltpu.VMEM((2, R, B), F32),
@@ -510,7 +553,7 @@
             pltpu.VMEM((N_COL, R, 2 * R), F32),
             pltpu.VMEM((B, B), BF16),
             pltpu.VMEM((NB, K, B), BF16),
-            pltpu.VMEM((NB + 2 * T, K, B), BF16),
+            pltpu.VMEM((NB + (NEAR - 1) * T, K, B), BF16),
             pltpu.VMEM((N_COL, R, 2 * R), BF16),
             pltpu.VMEM((NG, L, B), BF16),
             pltpu.VMEM((NG, L, WIDE), BF16),
@@ -518,14 +561,14 @@
             pltpu.VMEM((NG, R, L), BF16),
             pltpu.VMEM((NG, R, L), BF16),
             pltpu.VMEM((R, B), BF16),
-            pltpu.VMEM((2, R, B), BF16),
+            pltpu.VMEM((2, R, B), F32),
             pltpu.VMEM((T, NG, L, WIDE), BF16),
             pltpu.VMEM((T, T, L, WIDE), BF16),
             pltpu.VMEM((T, R, WIDE), F32),
             pltpu.VMEM((NG, T, R, L), BF16),
             pltpu.VMEM((NG, T, R, L), BF16),
             pltpu.VMEM((NG, T, R, L), BF16),
-            dma((4,)), dma((2,)), dma((2, BC)), dma((2, BC)), dma((2,)), dma((N_COL,)),
+            dma((4,)), dma((1,)), dma((2,)), dma((2, BC)), dma((2, BC)), dma((2,)), dma((N_COL,)),
             dma((NG,)), dma((T,)), dma((1,)), dma((NG,)), dma((NG,)), dma((NG, T)), dma((NG, T)), dma((N_COL,)),
             dma((N_COL,)), dma((NB,)), dma((NB,)), dma((N_COL,)), dma((N_COL,)),
             dma((T, NG)), dma((T, T)), dma((T,)), dma((NG, T)), dma((NG,)), dma((NG,)), dma((2,)),
@@ -535,7 +578,7 @@
         tile_ranks[:, 0, :, 0], rhs[:, 0], jnp.swapaxes(inverse_t[:, 0], 1, 2),
         u_factors[:, 0, :, 0], v_factors[:, 0, :, 0],
     )
-    return solved[:, None]
+    return (z - c.astype(F32))[:, None]
 
 
 def solution(mesh):

time: 57 us -> 55.8 us (0.979)
  other arithmetic: 0 us -> 1.72 us
  local copies, waits for them, and re-layouts: 1.67 us -> 0 us
  Pallas kernels: 55.2 us -> 53.9 us
    broadcast_in_dim x0 -> x1, other arithmetic: none -> 1.72 us  [on_device(): return (z - c.astype(F32))[:, None]]
    unnamed x1 -> x0, local copies, waits for them, and re-layouts: 1.67 us -> none
    pallas_call x1, Pallas kernels: 55.2 us -> 53.9 us  [on_device(): pl.pallas_call(kernel, out_shape=(jax.ShapeDtypeStruct((2, R, B), F32), j...]
where the time goes in v4:
time: 55.8 us; the launch traced here: 55.7 us
  Pallas kernels  53.9 us (97%)
  other arithmetic  1.72 us (3%)
    pallas_call x1, Pallas kernels, on_device(): pl.pallas_call(kernel, out_shape=(jax.ShapeDtypeStruct((2, R, B), F32), j...  53.9 us
    broadcast_in_dim x1, other arithmetic, on_device(): return (z - c.astype(F32))[:, None]  1.72 us

profile of v4, /device:TPU:27, one launch (start us, length us, event | category | flops | bytes accessed | tf_op | source)
XLA Modules:
  0.0 55.7 jit_solution(5932663929717285523)
XLA Ops:
  0.0 53.9 %shard_map.55 = (f32[2,64,512]{2,1,0:T(8,128)}, bf16[2,64,512]{2,1,0:T(8,128)(2,1)}) custom-call(s32[2,4]{1,0:T(2,128)} %bitcast.15, f32[2,64,512]{2,1,0:T(8,128)} %bitcast.11, f32[2,64,512]{2,1,0:T(8,128)} %bitcast.12, bf16[2,4,32,512]{3,2,1,0:T(8,128)(2,1)} %bitcast.13, bf16[2,4,32,512]{3,2,1,0:T(8,128)(2,1)} %bitcast.14), custom_call_target="tpu_custom_call" | custom-call | tf_op jit(solution)/shard_map/pallas_call | solution.py:539
  54.0 1.7 %subtract_bitcast_fusion = f32[2,1,64,512]{3,2,1,0:T(8,128)} fusion(f32[2,64,512]{2,1,0:T(8,128)} %get-tuple-element.7, bf16[2,64,512]{2,1,0:T(8,128)(2,1)} %get-tuple-element.8), kind=kLoop, calls=%fused_computation | loop fusion | flops 131072 | bytes 655360 | tf_op jit(solution)/shard_map/broadcast_in_dim | solution.py:581

commit v5 on v4

--- a/solution.py
+++ b/solution.py
@@ -37,7 +37,8 @@
 
 def chain_place(g):
     late = g // 4
-    return ((g + 3 * late) % 4) * 4 + 1 + late, 2 * (1 + late) + 1
+    row = ((g + 0 * late) % 4) * 4 + 1 + 1 * late
+    return row, 2 * (1 + 1 * late) + 1
 
 
 def kernel(
@@ -58,9 +59,10 @@
     is_row = q_odd & ((x_here - (r % 8) // 2) % 2 == 0)
     g_row = j_here // T
     t_row = j_here % T
-    late_chain = jnp.where(r % 4 == 2, 1, 0)
-    g_here = (r // 4 + late_chain) % 4 + 4 * late_chain
-    is_chain = q_odd & (x_here == 1 + late_chain) & (r % 4 == 1 + late_chain)
+    z_here = r % 4
+    late_chain = jnp.where((z_here == 2) & (x_here == 2), 1, 0)
+    g_here = (r // 4 + 0 * late_chain) % 4 + 4 * late_chain
+    is_chain = q_odd & (((z_here == 1) & (x_here == 1)) | (late_chain == 1))
 
     def is_me(row, col):
         return (row == r) & (col == q)
@@ -322,8 +324,8 @@
             z_full[a] = jnp.concatenate([zf[col][:, a * R:(a + 1) * R] for col in range(N_COL)], axis=1)
         pltpu.make_async_copy(z_full, z_out, out_s.at[0]).start()
 
-    def p_chain_copy(g):
-        return (p_out.at[g], p_in.at[g_here], pc_s.at[g], pc_r.at[g_here], *chain_place(g))
+    def p_chain_copy(g, i):
+        return (p_out.at[g, i], p_in.at[g_here, i], pc_s.at[g, i], pc_r.at[g_here, i], *chain_place(g))
 
     def p_row_copy(g, i):
         return (p_out.at[g, i], p_row.at[g_here], pr_s.at[g, i], pr_r.at[g_here], *row_place(g * T + i))
@@ -394,16 +396,20 @@
 
         @pl.loop(jnp.maximum(g_here - NEAR + 1, 0), g_here - 1)
         def _(lb):
-            arrived(p_in.at[lb], pc_r.at[lb])
+            for i in range(T):
+                arrived(p_in.at[lb, i], pc_r.at[lb, i])
             update(lb)
 
         @pl.when(g_here > 0)
         def _():
             wait_m(last)
-            arrived(p_in.at[last], pc_r.at[last])
 
         found, inner = [], []
         for t in range(T):
+            @pl.when(g_here > 0)
+            def _(t=t):
+                arrived(p_in.at[last, t], pc_r.at[last, t])
+
             x = acc[t, :, now] - nn(p_in[last, t], m_in[t, last, :, now])
             for s in range(t):
                 x = x - nn(inner[s], m_own[s, t, :, now])
@@ -414,7 +420,7 @@
         def _():
             for i, block in enumerate(across([x[:, L:] for x in found])):
                 p_out[g_here + 1, i] = block.astype(BF16)
-            remote(*p_chain_copy(g_here + 1)).start()
+                remote(*p_chain_copy(g_here + 1, i)).start()
 
         for i, block in enumerate(across([x[:, :L] for x in found])):
             if i > 0:
@@ -438,7 +444,7 @@
                     later.append(x)
                 for i, block in enumerate(across(later)):
                     p_out[g_here + ahead, i] = block.astype(BF16)
-                remote(*p_chain_copy(g_here + ahead)).start()
+                    remote(*p_chain_copy(g_here + ahead, i)).start()
                 for i in range(T):
                     remote(*p_row_copy(g_here + ahead, i)).start()
 
@@ -448,11 +454,12 @@
 
         blocks = g_row + jnp.where(t_row > 0, 1, 0)
 
-        def send_slabs():
-            @pl.loop(g_row + NEAR, NG)
-            def _(far):
-                s_out[far] = g_out[:, lanes_of(far, 1)].astype(BF16)
-                remote(*slab_copy(far)).start()
+        def send_slabs(h):
+            for far in (g_row + NEAR + 2 * h, g_row + NEAR + 2 * h + 1):
+                @pl.when(far < NG)
+                def _(far=far):
+                    s_out[far] = g_out[:, lanes_of(far, 1)].astype(BF16)
+                    remote(*slab_copy(far)).start()
 
         def term(g):
             arrived(p_row.at[g], pr_r.at[g])
@@ -463,15 +470,15 @@
                 cols = lanes_of(g_row + NEAR + 2 * h, 2)
                 g_out[:, cols] = g_out[:, cols] - nn(p, m_out[g, :, cols])
 
-            @pl.when(g == blocks - 1)
-            def _():
-                send_slabs()
+                @pl.when(g == blocks - 1)
+                def _():
+                    send_slabs(h)
 
             return nn(p, w[g])
 
         @pl.when(blocks == 0)
         def _():
-            send_slabs()
+            pl.loop(0, (NG - NEAR + 1 - g_row) // 2)(send_slabs)
 
         correction = lax.fori_loop(0, blocks, lambda g, total: total + term(g), jnp.zeros((R, B), F32))
         c_out[...] = correction.astype(BF16)
@@ -525,7 +532,8 @@
 
         @pl.loop(g_here + 1, upto)
         def _(g):
-            remote(*p_chain_copy(g)).wait_send()
+            for i in range(T):
+                remote(*p_chain_copy(g, i)).wait_send()
 
         @pl.loop(0, g_here - NEAR + 1)
         def _(lb):
@@ -569,9 +577,9 @@
             pltpu.VMEM((NG, T, R, L), BF16),
             pltpu.VMEM((NG, T, R, L), BF16),
             dma((4,)), dma((1,)), dma((2,)), dma((2, BC)), dma((2, BC)), dma((2,)), dma((N_COL,)),
-            dma((NG,)), dma((T,)), dma((1,)), dma((NG,)), dma((NG,)), dma((NG, T)), dma((NG, T)), dma((N_COL,)),
+            dma((NG,)), dma((T,)), dma((1,)), dma((NG,)), dma((NG, T)), dma((NG, T)), dma((NG, T)), dma((N_COL,)),
             dma((N_COL,)), dma((NB,)), dma((NB,)), dma((N_COL,)), dma((N_COL,)),
-            dma((T, NG)), dma((T, T)), dma((T,)), dma((NG, T)), dma((NG,)), dma((NG,)), dma((2,)),
+            dma((T, NG)), dma((T, T)), dma((T,)), dma((NG, T)), dma((NG, T)), dma((NG,)), dma((2,)),
         ],
         compiler_params=pltpu.CompilerParams(has_side_effects=True, collective_id=0),
     )(

time: 55.8 us -> 53.7 us (0.962)
  Pallas kernels: 53.9 us -> 51.8 us
    pallas_call x1, Pallas kernels: 53.9 us -> 51.8 us  [on_device(): pl.pallas_call(kernel, out_shape=(jax.ShapeDtypeStruct((2, R, B), F32), j...]
where the time goes in v5:
time: 53.7 us; the launch traced here: 53.5 us
  Pallas kernels  51.8 us (96%)
  other arithmetic  1.72 us (3%)
    pallas_call x1, Pallas kernels, on_device(): pl.pallas_call(kernel, out_shape=(jax.ShapeDtypeStruct((2, R, B), F32), j...  51.8 us
    broadcast_in_dim x1, other arithmetic, on_device(): return (z - c.astype(F32))[:, None]  1.72 us

profile of v5, /device:TPU:27, one launch (start us, length us, event | category | flops | bytes accessed | tf_op | source)
XLA Modules:
  0.0 53.5 jit_solution(12098266134715423318)
XLA Ops:
  0.0 51.8 %shard_map.55 = (f32[2,64,512]{2,1,0:T(8,128)}, bf16[2,64,512]{2,1,0:T(8,128)(2,1)}) custom-call(s32[2,4]{1,0:T(2,128)} %bitcast.15, f32[2,64,512]{2,1,0:T(8,128)} %bitcast.11, f32[2,64,512]{2,1,0:T(8,128)} %bitcast.12, bf16[2,4,32,512]{3,2,1,0:T(8,128)(2,1)} %bitcast.13, bf16[2,4,32,512]{3,2,1,0:T(8,128)(2,1)} %bitcast.14), custom_call_target="tpu_custom_call" | custom-call | tf_op jit(solution)/shard_map/pallas_call | solution.py:547
  51.8 1.7 %subtract_bitcast_fusion = f32[2,1,64,512]{3,2,1,0:T(8,128)} fusion(f32[2,64,512]{2,1,0:T(8,128)} %get-tuple-element.7, bf16[2,64,512]{2,1,0:T(8,128)(2,1)} %get-tuple-element.8), kind=kLoop, calls=%fused_computation | loop fusion | flops 131072 | bytes 655360 | tf_op jit(solution)/shard_map/broadcast_in_dim | solution.py:589

commit v6 on v5

--- a/solution.py
+++ b/solution.py
@@ -135,23 +135,23 @@
     def inv_copy(a):
         return (
             invt.at[a], inv_all.at[pl.ds(pl.multiple_of(q * R, R), R)],
-            inv_s.at[a], inv_r.at[q], *row_place(N_ROW * a + r),
+            inv_s.at[a], inv_r.at[0], *row_place(N_ROW * a + r),
         )
 
     def u_copy(a, c):
-        return (um.at[a, c], u_all.at[8 * c + q], u_s.at[a, c], u_r.at[8 * c + q], *row_place(N_ROW * a + r))
+        return (um.at[a, c], u_all.at[8 * c + q], u_s.at[a, c], u_r.at[(8 * c + q) // T], *row_place(N_ROW * a + r))
 
     def v_copy(a, c):
-        return (v.at[a, c], v_all.at[N_ROW * a + r], v_s.at[a, c], v_r.at[N_ROW * a + r], *row_place(8 * c + q))
+        return (v.at[a, c], v_all.at[N_ROW * a + r], v_s.at[a, c], v_r.at[(N_ROW * a + r) // T], *row_place(8 * c + q))
 
     def below(a, c):
         return 8 * c + q < N_ROW * a + r
 
     def zb_copy(a):
-        return (zpb.at[a], z_all.at[q], zb_s.at[a], zb_r.at[q], *row_place(N_ROW * a + r))
+        return (zpb.at[a], z_all.at[q], zb_s.at[a], zb_r.at[0], *row_place(N_ROW * a + r))
 
     def zf_copy(step):
-        return (zp, zf.at[q], zf_s.at[step], zf_r.at[q], r, (q + step) % N_COL)
+        return (zp, zf.at[q], zf_s.at[0], zf_r.at[0], r, (q + step) % N_COL)
 
     loads = [
         pltpu.make_async_copy(src, dst, in_s.at[k])
@@ -229,7 +229,7 @@
         lanes = lanes_of(g_row, count)
         return (
             m_out.at[lb, :, lanes], m_in.at[t_row, lb, :, lanes],
-            m_s.at[lb], m_r.at[t_row, lb], *chain_place(g_row),
+            m_s.at[lb], m_r.at[lb], *chain_place(g_row),
         )
 
     def own_copy(s, count):
@@ -237,38 +237,41 @@
         return (
             m_out.at[g_row, pl.ds(s * K, K), lanes],
             m_own.at[s, t_row, pl.ds(pl.multiple_of(t_row * K, K), K), lanes],
-            own_s.at[s], own_r.at[s, t_row], *chain_place(g_row),
+            own_s.at[s], own_r.at[0], *chain_place(g_row),
         )
 
     def g_copy(count):
         lanes = lanes_of(g_row, count)
         return (
             g_out.at[:, lanes], acc.at[t_row, :, lanes],
-            g_s.at[0], g_r.at[t_row], *chain_place(g_row),
+            g_s.at[0], g_r.at[0], *chain_place(g_row),
         )
 
     def slab_copy(g):
-        return (s_out.at[g], s_in.at[g_row, t_row], s_s.at[g], s_r.at[g_row, t_row], *chain_place(g))
+        return (s_out.at[g], s_in.at[g_row, t_row], s_s.at[g], s_r.at[g_row], *chain_place(g))
 
     def c_copy(col):
-        return (c_out, c_in.at[j_here // N_ROW], c_s.at[col], c_r.at[j_here // N_ROW], r, col)
+        return (c_out, c_in.at[j_here // N_ROW], c_s.at[0], c_r.at[j_here // N_ROW], r, col)
 
     @pl.when(is_row)
     def _():
         here = lanes_of(g_row, NEAR)
-        near_end = jnp.minimum((g_row + NEAR) * T, NB)
         rows = lax.broadcasted_iota(jnp.int32, (L, 1), 0) // K
 
         @pl.loop(g_row * T, j_here + 1)
         def _(i):
             v_all[i] = jnp.zeros((K, B), BF16)
 
-        for col in range(N_COL):
-            arrived(z_all.at[col], zb_r.at[col])
-
-        @pl.loop(j_here + 1, near_end)
-        def _(i):
-            arrived(v_all.at[i], v_r.at[i])
+        arrived(z_all, zb_r.at[0])
+
+        for t in range(T - 1):
+            @pl.when(t_row == t)
+            def _(t=t):
+                arrived(v_all.at[pl.ds(j_here + 1, T - 1 - t)], v_r.at[g_row])
+
+        @pl.loop(g_row + 1, jnp.minimum(g_row + NEAR, NG))
+        def _(g):
+            arrived(v_all.at[pl.ds(g * T, T)], v_r.at[g])
 
         def z():
             return jnp.concatenate([z_all[2 * h] + z_all[2 * h + 1] for h in range(N_COL // 2)], axis=1)
@@ -279,13 +282,13 @@
         g_out[:, here] = nt(z(), v_of(g_row, NEAR))
         by_width(g_row, lambda count: remote(*g_copy(count)).start())
 
-        for col in range(N_COL):
-            arrived(inv_all.at[pl.ds(col * R, R)], inv_r.at[col])
+        arrived(inv_all, inv_r.at[0])
 
         def form(lb):
-            @pl.loop(0, jnp.minimum(T, j_here - lb * T))
-            def _(l):
-                arrived(u_all.at[lb * T + l], u_r.at[lb * T + l])
+            for count in range(1, T + 1):
+                @pl.when(jnp.minimum(T, j_here - lb * T) == count)
+                def _(count=count):
+                    arrived(u_all.at[pl.ds(lb * T, count)], u_r.at[lb])
 
             wl = nt(u_all[pl.ds(lb * T, T)].reshape(L, B), inv_all[...])
             wl = jnp.where(rows + lb * T < j_here, wl, 0.0).astype(BF16)
@@ -303,9 +306,9 @@
             form(lb)
             by_width(g_row, lambda count: remote(*m_copy(lb, count)).start())
 
-        @pl.loop(near_end, NB)
-        def _(i):
-            arrived(v_all.at[i], v_r.at[i])
+        @pl.loop(g_row + NEAR, NG)
+        def _(g):
+            arrived(v_all.at[pl.ds(g * T, T)], v_r.at[g])
 
         @pl.loop(0, (NG - NEAR + 1 - g_row) // 2)
         def _(h):
@@ -318,20 +321,19 @@
                 m_out[lb, :, cols] = nt(w[lb], v_of(far, 2)).astype(BF16)
 
     def join_z():
-        for col in range(N_COL):
-            arrived(zf.at[col], zf_r.at[col])
+        arrived(zf, zf_r.at[0])
         for a in range(2):
             z_full[a] = jnp.concatenate([zf[col][:, a * R:(a + 1) * R] for col in range(N_COL)], axis=1)
         pltpu.make_async_copy(z_full, z_out, out_s.at[0]).start()
 
     def p_chain_copy(g, i):
-        return (p_out.at[g, i], p_in.at[g_here, i], pc_s.at[g, i], pc_r.at[g_here, i], *chain_place(g))
+        return (p_out.at[g, i], p_in.at[g_here, i], pc_s.at[g], pc_r.at[g - g_here - 1, i], *chain_place(g))
 
     def p_row_copy(g, i):
-        return (p_out.at[g, i], p_row.at[g_here], pr_s.at[g, i], pr_r.at[g_here], *row_place(g * T + i))
+        return (p_out.at[g, i], p_row.at[g_here], pr_s.at[g], pr_r.at[g_here], *row_place(g * T + i))
 
     def relay_copy(lb, i):
-        return (p_in.at[lb, i], p_row.at[lb], relay_s.at[lb, i], pr_r.at[lb], *row_place(g_here * T + i))
+        return (p_in.at[lb, i], p_row.at[lb], relay_s.at[lb], pr_r.at[lb], *row_place(g_here * T + i))
 
     @pl.when(is_chain)
     def _():
@@ -364,11 +366,7 @@
         now = lanes_of(g_here, 2)
 
         def wait_m(lb):
-            def of(count):
-                for t in range(T):
-                    arrived(m_in.at[t, lb, :, lanes_of(g_here, count)], m_r.at[t, lb])
-
-            by_width(g_here, of)
+            by_width(g_here, lambda count: arrived(m_in.at[:, lb, :, lanes_of(g_here, count)], m_r.at[lb]))
 
         def update(lb):
             wait_m(lb)
@@ -377,17 +375,14 @@
 
         def wait_start(count):
             lanes = lanes_of(g_here, count)
-            for t in range(T):
-                arrived(acc.at[t, :, lanes], g_r.at[t])
-                for s in range(t):
-                    arrived(m_own.at[s, t, pl.ds(t * K, K), lanes], own_r.at[s, t])
+            arrived(acc.at[:, :, lanes], g_r.at[0])
+            arrived(m_own.at[0, pl.ds(0, 2), pl.ds(0, 3 * K), lanes], own_r.at[0])
 
         by_width(g_here, wait_start)
 
         @pl.loop(0, g_here - NEAR + 1)
         def _(lb):
-            for t in range(T):
-                arrived(s_in.at[lb, t], s_r.at[lb, t])
+            arrived(s_in.at[lb], s_r.at[lb])
             for i, block in enumerate(across([s_in[lb, t].astype(F32) for t in range(T)])):
                 p_in[lb, i] = block.astype(BF16)
             for i in range(T):
@@ -397,7 +392,7 @@
         @pl.loop(jnp.maximum(g_here - NEAR + 1, 0), g_here - 1)
         def _(lb):
             for i in range(T):
-                arrived(p_in.at[lb, i], pc_r.at[lb, i])
+                arrived(p_in.at[lb, i], pc_r.at[g_here - lb - 1, i])
             update(lb)
 
         @pl.when(g_here > 0)
@@ -408,7 +403,7 @@
         for t in range(T):
             @pl.when(g_here > 0)
             def _(t=t):
-                arrived(p_in.at[last, t], pc_r.at[last, t])
+                arrived(p_in.at[last, t], pc_r.at[0, t])
 
             x = acc[t, :, now] - nn(p_in[last, t], m_in[t, last, :, now])
             for s in range(t):
@@ -496,8 +491,7 @@
     each_u(sent, 0)
     second_wave(sent)
     each_v(sent, False, range(BC))
-    for step in range(1, N_COL):
-        sent(*zf_copy(step))
+    arrived(zf.at[pl.ds(0, N_COL - 1)], zf_s.at[0])
 
     @pl.when(is_row)
     def _():
@@ -515,30 +509,22 @@
         def _(far):
             remote(*slab_copy(far)).wait_send()
 
-        for col in range(N_COL):
-            sent(*c_copy(col))
+        arrived(p_out.at[pl.ds(0, N_COL - 1)], c_s.at[0])
 
     @pl.when(is_chain)
     def _():
         upto = jnp.minimum(g_here + NEAR, NG)
 
-        for i in range(1, T):
-            remote(*p_row_copy(g_here, i)).wait_send()
+        arrived(p_out.at[g_here, pl.ds(1, T - 1)], pr_s.at[g_here])
 
         @pl.loop(g_here + 1, upto)
         def _(g):
-            for i in range(T):
-                remote(*p_row_copy(g, i)).wait_send()
-
-        @pl.loop(g_here + 1, upto)
-        def _(g):
-            for i in range(T):
-                remote(*p_chain_copy(g, i)).wait_send()
+            arrived(p_out.at[g], pr_s.at[g])
+            arrived(p_out.at[g], pc_s.at[g])
 
         @pl.loop(0, g_here - NEAR + 1)
         def _(lb):
-            for i in range(T):
-                remote(*relay_copy(lb, i)).wait_send()
+            arrived(p_in.at[lb], relay_s.at[lb])
 
 
 def on_device(rhs, inverse_t, u_factors, v_factors, tile_ranks):
@@ -576,10 +562,10 @@
             pltpu.VMEM((NG, T, R, L), BF16),
             pltpu.VMEM((NG, T, R, L), BF16),
             pltpu.VMEM((NG, T, R, L), BF16),
-            dma((4,)), dma((1,)), dma((2,)), dma((2, BC)), dma((2, BC)), dma((2,)), dma((N_COL,)),
-            dma((NG,)), dma((T,)), dma((1,)), dma((NG,)), dma((NG, T)), dma((NG, T)), dma((NG, T)), dma((N_COL,)),
-            dma((N_COL,)), dma((NB,)), dma((NB,)), dma((N_COL,)), dma((N_COL,)),
-            dma((T, NG)), dma((T, T)), dma((T,)), dma((NG, T)), dma((NG, T)), dma((NG,)), dma((2,)),
+            dma((4,)), dma((1,)), dma((2,)), dma((2, BC)), dma((2, BC)), dma((2,)), dma((1,)),
+            dma((NG,)), dma((T,)), dma((1,)), dma((NG,)), dma((NG,)), dma((NG,)), dma((NG,)), dma((1,)),
+            dma((1,)), dma((NG,)), dma((NG,)), dma((1,)), dma((1,)),
+            dma((NG,)), dma((1,)), dma((1,)), dma((NG,)), dma((2, T)), dma((NG,)), dma((2,)),
         ],
         compiler_params=pltpu.CompilerParams(has_side_effects=True, collective_id=0),
     )(

time: 53.7 us -> 51.4 us (0.957)
  Pallas kernels: 51.8 us -> 49.5 us
    pallas_call x1, Pallas kernels: 51.8 us -> 49.5 us  [on_device(): pl.pallas_call(kernel, out_shape=(jax.ShapeDtypeStruct((2, R, B), F32), j...]
where the time goes in v6:
time: 51.4 us; the launch traced here: 51.3 us
  Pallas kernels  49.5 us (96%)
  other arithmetic  1.72 us (3%)
    pallas_call x1, Pallas kernels, on_device(): pl.pallas_call(kernel, out_shape=(jax.ShapeDtypeStruct((2, R, B), F32), j...  49.5 us
    broadcast_in_dim x1, other arithmetic, on_device(): return (z - c.astype(F32))[:, None]  1.72 us

profile of v6, /device:TPU:27, one launch (start us, length us, event | category | flops | bytes accessed | tf_op | source)
XLA Modules:
  0.0 51.3 jit_solution(12808155448045563941)
XLA Ops:
  0.0 49.5 %shard_map.55 = (f32[2,64,512]{2,1,0:T(8,128)}, bf16[2,64,512]{2,1,0:T(8,128)(2,1)}) custom-call(s32[2,4]{1,0:T(2,128)} %bitcast.15, f32[2,64,512]{2,1,0:T(8,128)} %bitcast.11, f32[2,64,512]{2,1,0:T(8,128)} %bitcast.12, bf16[2,4,32,512]{3,2,1,0:T(8,128)(2,1)} %bitcast.13, bf16[2,4,32,512]{3,2,1,0:T(8,128)(2,1)} %bitcast.14), custom_call_target="tpu_custom_call" | custom-call | tf_op jit(solution)/shard_map/pallas_call | solution.py:533
  49.5 1.7 %subtract_bitcast_fusion = f32[2,1,64,512]{3,2,1,0:T(8,128)} fusion(f32[2,64,512]{2,1,0:T(8,128)} %get-tuple-element.7, bf16[2,64,512]{2,1,0:T(8,128)(2,1)} %get-tuple-element.8), kind=kLoop, calls=%fused_computation | loop fusion | flops 131072 | bytes 655360 | tf_op jit(solution)/shard_map/broadcast_in_dim | solution.py:575

commit v7 on v6

--- a/solution.py
+++ b/solution.py
@@ -209,7 +209,6 @@
     mask_u(0)
     each_u(send, 0)
     mask_u(1)
-    first_wave(sent)
     each_v(send, False, (0,))
     second_wave(send)
     each_v(send, False, (1, 2, 3))
@@ -225,26 +224,38 @@
             def _(count=count):
                 do(count)
 
-    def m_copy(lb, count):
-        lanes = lanes_of(g_row, count)
+    def by_need(do):
+        def of(count):
+            @pl.when(t_row < T - 1)
+            def _():
+                do(lanes_of(g_row, count))
+
+            if count > 1:
+                @pl.when(t_row == T - 1)
+                def _():
+                    do(lanes_of(g_row + 1, count - 1))
+
+        by_width(g_row, of)
+
+    half = jnp.where(t_row == T - 1, 1, 0)
+
+    def m_copy(lb, lanes):
         return (
             m_out.at[lb, :, lanes], m_in.at[t_row, lb, :, lanes],
-            m_s.at[lb], m_r.at[lb], *chain_place(g_row),
+            m_s.at[lb], m_r.at[half, lb], *chain_place(g_row),
         )
 
-    def own_copy(s, count):
-        lanes = lanes_of(g_row, count)
+    def own_copy(s, lanes):
         return (
             m_out.at[g_row, pl.ds(s * K, K), lanes],
             m_own.at[s, t_row, pl.ds(pl.multiple_of(t_row * K, K), K), lanes],
-            own_s.at[s], own_r.at[0], *chain_place(g_row),
+            own_s.at[s], own_r.at[half], *chain_place(g_row),
         )
 
-    def g_copy(count):
-        lanes = lanes_of(g_row, count)
+    def g_copy(lanes):
         return (
             g_out.at[:, lanes], acc.at[t_row, :, lanes],
-            g_s.at[0], g_r.at[0], *chain_place(g_row),
+            g_s.at[0], g_r.at[half], *chain_place(g_row),
         )
 
     def slab_copy(g):
@@ -280,7 +291,7 @@
             return v_all[pl.ds(g * T, count * T)].reshape(count * L, B)
 
         g_out[:, here] = nt(z(), v_of(g_row, NEAR))
-        by_width(g_row, lambda count: remote(*g_copy(count)).start())
+        by_need(lambda lanes: remote(*g_copy(lanes)).start())
 
         arrived(inv_all, inv_r.at[0])
 
@@ -299,12 +310,12 @@
 
         @pl.loop(0, t_row)
         def _(s):
-            by_width(g_row, lambda count: remote(*own_copy(s, count)).start())
+            by_need(lambda lanes: remote(*own_copy(s, lanes)).start())
 
         @pl.loop(0, g_row)
         def _(lb):
             form(lb)
-            by_width(g_row, lambda count: remote(*m_copy(lb, count)).start())
+            by_need(lambda lanes: remote(*m_copy(lb, lanes)).start())
 
         @pl.loop(g_row + NEAR, NG)
         def _(g):
@@ -366,7 +377,12 @@
         now = lanes_of(g_here, 2)
 
         def wait_m(lb):
-            by_width(g_here, lambda count: arrived(m_in.at[:, lb, :, lanes_of(g_here, count)], m_r.at[lb]))
+            def of(count):
+                arrived(m_in.at[pl.ds(0, T - 1), lb, :, lanes_of(g_here, count)], m_r.at[0, lb])
+                if count > 1:
+                    arrived(m_in.at[T - 1, lb, :, lanes_of(g_here + 1, count - 1)], m_r.at[1, lb])
+
+            by_width(g_here, of)
 
         def update(lb):
             wait_m(lb)
@@ -375,8 +391,12 @@
 
         def wait_start(count):
             lanes = lanes_of(g_here, count)
-            arrived(acc.at[:, :, lanes], g_r.at[0])
-            arrived(m_own.at[0, pl.ds(0, 2), pl.ds(0, 3 * K), lanes], own_r.at[0])
+            arrived(acc.at[pl.ds(0, T - 1), :, lanes], g_r.at[0])
+            arrived(m_own.at[0, 0, pl.ds(0, 3 * K), lanes], own_r.at[0])
+            if count > 1:
+                lanes = lanes_of(g_here + 1, count - 1)
+                arrived(acc.at[T - 1, :, lanes], g_r.at[1])
+                arrived(m_own.at[0, 0, pl.ds(0, 3 * K), lanes], own_r.at[1])
 
         by_width(g_here, wait_start)
 
@@ -488,6 +508,7 @@
     for a in range(2):
         arrived(c_in.at[a], c_r.at[a])
 
+    first_wave(sent)
     each_u(sent, 0)
     second_wave(sent)
     each_v(sent, False, range(BC))
@@ -495,15 +516,15 @@
 
     @pl.when(is_row)
     def _():
-        by_width(g_row, lambda count: remote(*g_copy(count)).wait_send())
+        by_need(lambda lanes: remote(*g_copy(lanes)).wait_send())
 
         @pl.loop(0, g_row)
         def _(lb):
-            by_width(g_row, lambda count: remote(*m_copy(lb, count)).wait_send())
+            by_need(lambda lanes: remote(*m_copy(lb, lanes)).wait_send())
 
         @pl.loop(0, t_row)
         def _(s):
-            by_width(g_row, lambda count: remote(*own_copy(s, count)).wait_send())
+            by_need(lambda lanes: remote(*own_copy(s, lanes)).wait_send())
 
         @pl.loop(g_row + NEAR, NG)
         def _(far):
@@ -565,7 +586,7 @@
             dma((4,)), dma((1,)), dma((2,)), dma((2, BC)), dma((2, BC)), dma((2,)), dma((1,)),
             dma((NG,)), dma((T,)), dma((1,)), dma((NG,)), dma((NG,)), dma((NG,)), dma((NG,)), dma((1,)),
             dma((1,)), dma((NG,)), dma((NG,)), dma((1,)), dma((1,)),
-            dma((NG,)), dma((1,)), dma((1,)), dma((NG,)), dma((2, T)), dma((NG,)), dma((2,)),
+            dma((2, NG)), dma((2,)), dma((2,)), dma((NG,)), dma((2, T)), dma((NG,)), dma((2,)),
         ],
         compiler_params=pltpu.CompilerParams(has_side_effects=True, collective_id=0),
     )(

time: 51.4 us -> 50.4 us (0.981)
  Pallas kernels: 49.5 us -> 48.5 us
    pallas_call x1, Pallas kernels: 49.5 us -> 48.5 us  [on_device(): pl.pallas_call(kernel, out_shape=(jax.ShapeDtypeStruct((2, R, B), F32), j...]
where the time goes in v7:
time: 50.4 us; the launch traced here: 50.2 us
  Pallas kernels  48.5 us (96%)
  other arithmetic  1.72 us (3%)
    pallas_call x1, Pallas kernels, on_device(): pl.pallas_call(kernel, out_shape=(jax.ShapeDtypeStruct((2, R, B), F32), j...  48.5 us
    broadcast_in_dim x1, other arithmetic, on_device(): return (z - c.astype(F32))[:, None]  1.72 us

profile of v7, /device:TPU:27, one launch (start us, length us, event | category | flops | bytes accessed | tf_op | source)
XLA Modules:
  0.0 50.2 jit_solution(7426801772648453805)
XLA Ops:
  0.0 48.5 %shard_map.55 = (f32[2,64,512]{2,1,0:T(8,128)}, bf16[2,64,512]{2,1,0:T(8,128)(2,1)}) custom-call(s32[2,4]{1,0:T(2,128)} %bitcast.15, f32[2,64,512]{2,1,0:T(8,128)} %bitcast.11, f32[2,64,512]{2,1,0:T(8,128)} %bitcast.12, bf16[2,4,32,512]{3,2,1,0:T(8,128)(2,1)} %bitcast.13, bf16[2,4,32,512]{3,2,1,0:T(8,128)(2,1)} %bitcast.14), custom_call_target="tpu_custom_call" | custom-call | tf_op jit(solution)/shard_map/pallas_call | solution.py:554
  48.5 1.7 %subtract_bitcast_fusion = f32[2,1,64,512]{3,2,1,0:T(8,128)} fusion(f32[2,64,512]{2,1,0:T(8,128)} %get-tuple-element.7, bf16[2,64,512]{2,1,0:T(8,128)(2,1)} %get-tuple-element.8), kind=kLoop, calls=%fused_computation | loop fusion | flops 131072 | bytes 655360 | tf_op jit(solution)/shard_map/broadcast_in_dim | solution.py:596

commit v8 on v7

--- a/solution.py
+++ b/solution.py
@@ -46,8 +46,8 @@
     rhs, inv, u, v, um, invt, zp, zpb, zf,
     inv_all, u_all, v_all, z_all, w, m_out, g_out, p_row, s_out, c_out, z_full,
     m_in, m_own, acc, s_in, p_in, p_out,
-    in_s, out_s, inv_s, u_s, v_s, zb_s, zf_s, m_s, own_s, g_s, s_s, pc_s, pr_s, relay_s, c_s,
-    inv_r, u_r, v_r, zb_r, zf_r, m_r, own_r, g_r, s_r, pc_r, pr_r, c_r,
+    in_s, out_s, inv_s, u_s, v_s, zb_s, zf_s, m_s, own_s, g_s, s_s, pc_s, c_s,
+    inv_r, u_r, v_r, zb_r, zf_r, m_r, own_r, g_r, pc_r, pr_r, c_r,
 ):
     r = lax.axis_index("row")
     q = lax.axis_index("col")
@@ -259,7 +259,7 @@
         )
 
     def slab_copy(g):
-        return (s_out.at[g], s_in.at[g_row, t_row], s_s.at[g], s_r.at[g_row], *chain_place(g))
+        return (s_out.at[g], s_in.at[g_row, t_row], s_s.at[g], u_r.at[g_row], *chain_place(g))
 
     def c_copy(col):
         return (c_out, c_in.at[j_here // N_ROW], c_s.at[0], c_r.at[j_here // N_ROW], r, col)
@@ -341,10 +341,10 @@
         return (p_out.at[g, i], p_in.at[g_here, i], pc_s.at[g], pc_r.at[g - g_here - 1, i], *chain_place(g))
 
     def p_row_copy(g, i):
-        return (p_out.at[g, i], p_row.at[g_here], pr_s.at[g], pr_r.at[g_here], *row_place(g * T + i))
+        return (p_out.at[g, i], p_row.at[g_here], m_s.at[g], pr_r.at[g_here], *row_place(g * T + i))
 
     def relay_copy(lb, i):
-        return (p_in.at[lb, i], p_row.at[lb], relay_s.at[lb], pr_r.at[lb], *row_place(g_here * T + i))
+        return (p_in.at[lb, i], p_row.at[lb], s_s.at[lb], pr_r.at[lb], *row_place(g_here * T + i))
 
     @pl.when(is_chain)
     def _():
@@ -402,7 +402,7 @@
 
         @pl.loop(0, g_here - NEAR + 1)
         def _(lb):
-            arrived(s_in.at[lb], s_r.at[lb])
+            arrived(s_in.at[lb], u_r.at[lb])
             for i, block in enumerate(across([s_in[lb, t].astype(F32) for t in range(T)])):
                 p_in[lb, i] = block.astype(BF16)
             for i in range(T):
@@ -536,16 +536,16 @@
     def _():
         upto = jnp.minimum(g_here + NEAR, NG)
 
-        arrived(p_out.at[g_here, pl.ds(1, T - 1)], pr_s.at[g_here])
+        arrived(p_out.at[g_here, pl.ds(1, T - 1)], m_s.at[g_here])
 
         @pl.loop(g_here + 1, upto)
         def _(g):
-            arrived(p_out.at[g], pr_s.at[g])
+            arrived(p_out.at[g], m_s.at[g])
             arrived(p_out.at[g], pc_s.at[g])
 
         @pl.loop(0, g_here - NEAR + 1)
         def _(lb):
-            arrived(p_in.at[lb], relay_s.at[lb])
+            arrived(p_in.at[lb], s_s.at[lb])
 
 
 def on_device(rhs, inverse_t, u_factors, v_factors, tile_ranks):
@@ -584,9 +584,9 @@
             pltpu.VMEM((NG, T, R, L), BF16),
             pltpu.VMEM((NG, T, R, L), BF16),
             dma((4,)), dma((1,)), dma((2,)), dma((2, BC)), dma((2, BC)), dma((2,)), dma((1,)),
-            dma((NG,)), dma((T,)), dma((1,)), dma((NG,)), dma((NG,)), dma((NG,)), dma((NG,)), dma((1,)),
+            dma((NG,)), dma((T,)), dma((1,)), dma((NG,)), dma((NG,)), dma((1,)),
             dma((1,)), dma((NG,)), dma((NG,)), dma((1,)), dma((1,)),
-            dma((2, NG)), dma((2,)), dma((2,)), dma((NG,)), dma((2, T)), dma((NG,)), dma((2,)),
+            dma((2, NG)), dma((2,)), dma((2,)), dma((2, T)), dma((NG,)), dma((2,)),
         ],
         compiler_params=pltpu.CompilerParams(has_side_effects=True, collective_id=0),
     )(

time: 50.4 us -> 50.2 us (level)
  no operation moved by 1% of the time
where the time goes in v8:
time: 50.2 us; the launch traced here: 50 us
  Pallas kernels  48.3 us (96%)
  other arithmetic  1.72 us (3%)
    pallas_call x1, Pallas kernels, on_device(): pl.pallas_call(kernel, out_shape=(jax.ShapeDtypeStruct((2, R, B), F32), j...  48.3 us
    broadcast_in_dim x1, other arithmetic, on_device(): return (z - c.astype(F32))[:, None]  1.72 us

profile of v8, /device:TPU:27, one launch (start us, length us, event | category | flops | bytes accessed | tf_op | source)
XLA Modules:
  0.0 50.0 jit_solution(6290615977340570721)
XLA Ops:
  0.0 48.3 %shard_map.55 = (f32[2,64,512]{2,1,0:T(8,128)}, bf16[2,64,512]{2,1,0:T(8,128)(2,1)}) custom-call(s32[2,4]{1,0:T(2,128)} %bitcast.15, f32[2,64,512]{2,1,0:T(8,128)} %bitcast.11, f32[2,64,512]{2,1,0:T(8,128)} %bitcast.12, bf16[2,4,32,512]{3,2,1,0:T(8,128)(2,1)} %bitcast.13, bf16[2,4,32,512]{3,2,1,0:T(8,128)(2,1)} %bitcast.14), custom_call_target="tpu_custom_call" | custom-call | tf_op jit(solution)/shard_map/pallas_call | solution.py:554
  48.3 1.7 %subtract_bitcast_fusion = f32[2,1,64,512]{3,2,1,0:T(8,128)} fusion(f32[2,64,512]{2,1,0:T(8,128)} %get-tuple-element.7, bf16[2,64,512]{2,1,0:T(8,128)(2,1)} %get-tuple-element.8), kind=kLoop, calls=%fused_computation | loop fusion | flops 131072 | bytes 655360 | tf_op jit(solution)/shard_map/broadcast_in_dim | solution.py:596
